TPU v7x, 32 devices: a whole 2x2x4 slice. The times are simulated.
32 devices in a mesh: rep: 2 (over core), seq: 16 (over z, y, x).
Axes of the slice: x: 2, y: 2, z: 4, core: 2. Of those that a mesh axis runs over, the one named last changes fastest.
Arguments:
- queries: bfloat16 [4096, 8192], P(('rep', 'seq')), parts along dimension 0, may hold values from -180 to 180
- keys: bfloat16 [16384, 1024], P(('rep', 'seq')), parts along dimension 0, may hold values from -6 to 6
- values: bfloat16 [16384, 1024], P(('rep', 'seq')), parts along dimension 0, may hold values from -6 to 6
- vertical: int32 [128, 64], P('rep'), parts along dimension 0, may hold values from 0 to 127, all different within a row
- vert_count: int32 [128], P('rep'), parts along dimension 0, may hold values from 1 to 64
- slash: int32 [128, 32], P('rep'), parts along dimension 0, may hold values from 0 to 95, all different within a row
- slash_count: int32 [128], P('rep'), parts along dimension 0, may hold values from 1 to 32
Outputs:
- attended: bfloat16 [4096, 8192], P(('rep', 'seq')), parts along dimension 0
There are 2 independent parts, one for each index of `rep`. A program takes and returns all parts, laid end to end along the dimension named above; each array names one. Nothing has to cross between parts.
Inputs may be any that keep to these rules, and one draw needn't show every extreme that they name: `vertical`: each row holds 64 different key block numbers; head h uses the first vert_count[h] of them. `slash`: each row holds 32 different numbers; head h uses the first slash_count[h] of them, each number s naming the slash offset s + 1 blocks.
All inputs are finite; a program needn't handle non-finite values.
Results may differ from a plain program's by a relative error of at most 0.007.
Values may be sent and summed in bfloat16 or wider, within the bound.
No kernel may reach another device: no remote copies, remote signals or barrier semaphores. Data moves between devices by JAX's collectives and lax.ppermute only.
A program may use at most 128 MiB of HBM per device.

v0:
```python
import functools
import math

import jax
import jax.numpy as jnp
from jax import lax
from jax.experimental import pallas as pl
from jax.experimental.pallas import tpu as pltpu
from jax.sharding import PartitionSpec as P


QUERY_HEADS = 64
KV_HEADS = 8
HEAD_DIM = 128
BLOCK = 64
LANES = 128
ONES = 16
HIDE = -1e30
STEPS = 4


def attention_kernel(factor, pieces, side_ref, table_ref, q_ref, *refs):
    cache_refs, (out_ref, keys, values, mask, qa, sa, sb, acc, sem) = refs[:2 * pieces], refs[-9:]
    head, tile = pl.program_id(0), pl.program_id(1)
    tiles = pl.num_programs(1)
    _, senders, piece_rows, _ = keys.shape
    chunk = pieces * piece_rows
    width = HEAD_DIM
    rows = q_ref.shape[0]
    piece_blocks = piece_rows // BLOCK
    copies = [pltpu.make_async_copy(cache_refs[p], keys.at[p], sem.at[p]) for p in range(pieces)]
    copies += [pltpu.make_async_copy(cache_refs[pieces + p], values.at[p], sem.at[pieces + p]) for p in range(pieces)]
    fresh = (head == 0) & (tile == 0)

    @pl.when(fresh)
    def _():
        for copy in copies:
            copy.start()

    @pl.when(tile == 0)
    def _():
        def fill(sender, carry):
            for p in range(pieces):
                block = (sender * pieces + (p ^ side_ref[0])) * piece_blocks
                for b in range(piece_blocks):
                    row = table_ref[0, pl.ds(block + b, 1), :]
                    at = pl.multiple_of(sender * chunk + (p * piece_blocks + b) * BLOCK, BLOCK)
                    mask[pl.ds(at, BLOCK), :] = jnp.broadcast_to(row, (BLOCK, row.shape[1])).astype(jnp.bfloat16)
            return carry

        lax.fori_loop(0, senders, fill, 0)

    qa[:width, :] = q_ref[...].T
    lane_block = lax.broadcasted_iota(jnp.int32, mask.shape[1:] + (rows,), 1) // BLOCK + tile * (rows // BLOCK)
    qa[width:, :] = (lax.broadcasted_iota(jnp.int32, lane_block.shape, 0) == lane_block).astype(jnp.float32).astype(jnp.bfloat16)
    acc[...] = jnp.zeros_like(acc)
    own = senders - tiles + tile
    count = own + 1

    @pl.when(fresh)
    def _():
        for copy in copies:
            copy.wait()

    def where_at(step):
        return jnp.where(step == 0, own, jnp.minimum(step - 1, own))

    def product(step):
        at = where_at(step)
        held = jnp.concatenate([keys[p, at] for p in range(pieces)], axis=0)
        bias = mask[pl.ds(pl.multiple_of(at * chunk, chunk), chunk), :]
        return jnp.dot(jnp.concatenate([held, bias], axis=1), qa[...], preferred_element_type=jnp.float32)

    def top_of(s):
        return jnp.max(s.reshape(chunk // 8, 8, rows), axis=0)

    def score(step, s_ref):
        s = product(step)
        s_ref[...] = s
        return top_of(s)

    def fold(step, s_ref, peak, part):
        top = jnp.maximum(peak, jnp.max(part, axis=0, keepdims=True))
        alpha = jnp.exp2((peak - top) * factor)
        p = jnp.exp2((s_ref[...] - top) * factor).astype(jnp.bfloat16)
        at = where_at(step)
        held = jnp.concatenate([values[i, at] for i in range(pieces)], axis=0)
        held = jnp.concatenate([held.T, jnp.ones((ONES, chunk), jnp.bfloat16)], axis=0)
        acc[...] = acc[...] * alpha + jnp.dot(held, p, preferred_element_type=jnp.float32)
        return top

    s = product(0)
    row = lax.broadcasted_iota(jnp.int32, s.shape, 0)
    row = (row // piece_rows ^ side_ref[0]) * piece_rows + row % piece_rows
    s = jnp.where(row <= lax.broadcasted_iota(jnp.int32, s.shape, 1), s, HIDE)
    sa[...] = s
    peak = jnp.full((1, rows), HIDE, jnp.float32)

    def pair(i, carry):
        peak, part = carry
        part_b = score(2 * i + 1, sb)
        peak = fold(2 * i, sa, peak, part)
        part = score(2 * i + 2, sa)
        peak = fold(2 * i + 1, sb, peak, part_b)
        return peak, part

    peak, part = lax.fori_loop(0, count // 2, pair, (peak, top_of(s)))

    @pl.when(count % 2 == 1)
    def _():
        fold(count - 1, sa, peak, part)

    total = acc[width:width + 1, :]
    out_ref[...] = (acc[:width, :] / total).T.astype(out_ref.dtype)


def attention(q, keys, values, table, side, first=0, place=0, breadth=1, prior=None):
    pieces = len(keys)
    senders, piece_rows, _ = keys[0].shape
    chunk = pieces * piece_rows
    tiles = q.shape[0] // chunk
    context = senders * chunk
    lanes = table.shape[2]
    factor = math.log2(math.e) / math.sqrt(HEAD_DIM)
    pairs = q.shape[0] * context
    priors = [] if prior is None else [prior]
    anywhere = pl.BlockSpec(memory_space=pl.ANY)
    return pl.pallas_call(
        functools.partial(attention_kernel, factor, pieces),
        out_shape=jax.ShapeDtypeStruct((q.shape[0], breadth * HEAD_DIM), jnp.bfloat16),
        grid_spec=pltpu.PrefetchScalarGridSpec(
            num_scalar_prefetch=1,
            grid=(1, tiles),
            in_specs=[
                pl.BlockSpec((1, table.shape[1], lanes), lambda h, t, s: (h, 0, 0)),
                pl.BlockSpec((chunk, HEAD_DIM), lambda h, t, s: (t, h + first)),
            ]
            + [anywhere] * (2 * pieces + len(priors)),
            out_specs=pl.BlockSpec((chunk, HEAD_DIM), lambda h, t, s: (t, h + place)),
            scratch_shapes=[
                pltpu.VMEM((pieces,) + keys[0].shape, jnp.bfloat16),
                pltpu.VMEM((pieces,) + values[0].shape, jnp.bfloat16),
                pltpu.VMEM((context, lanes), jnp.bfloat16),
                pltpu.VMEM((HEAD_DIM + lanes, chunk), jnp.bfloat16),
                pltpu.VMEM((chunk, chunk), jnp.float32),
                pltpu.VMEM((chunk, chunk), jnp.float32),
                pltpu.VMEM((HEAD_DIM + ONES, chunk), jnp.float32),
                pltpu.SemaphoreType.DMA((2 * pieces,)),
            ],
        ),
        compiler_params=pltpu.CompilerParams(
            dimension_semantics=("arbitrary", "arbitrary"), vmem_limit_bytes=67000000
        ),
        cost_estimate=pl.CostEstimate(
            flops=4 * pairs * HEAD_DIM,
            bytes_accessed=4 * q.shape[0] * HEAD_DIM + 4 * pieces * keys[0].size,
            transcendentals=pairs,
        ),
        input_output_aliases={3 + 2 * pieces: 0} if priors else {},
        name="attention",
    )(side, table, q, *keys, *values, *priors)


def pack_cache(x, sharers):
    rows, _ = x.shape
    piece_rows = rows // sharers
    some = KV_HEADS // STEPS

    def kernel(in_ref, out_ref):
        for g in range(some):
            for p in range(sharers):
                out_ref[g * sharers + p] = in_ref[p * piece_rows:(p + 1) * piece_rows, g * HEAD_DIM:(g + 1) * HEAD_DIM]

    return pl.pallas_call(
        kernel,
        out_shape=jax.ShapeDtypeStruct((KV_HEADS * sharers, piece_rows, HEAD_DIM), x.dtype),
        grid=(STEPS,),
        in_specs=[pl.BlockSpec((rows, some * HEAD_DIM), lambda i: (0, i))],
        out_specs=pl.BlockSpec((some * sharers, piece_rows, HEAD_DIM), lambda i: (i, 0, 0)),
        cost_estimate=pl.CostEstimate(flops=16 * x.size, bytes_accessed=4 * x.size, transcendentals=0),
        name="pack_cache",
    )(x)


def pack_queries(queries, devices, sizes):
    rows, width = queries.shape
    heads = sum(sizes)
    some = devices // STEPS

    def kernel(q_ref, *out_refs):
        for d in range(some):
            head = 0
            for size, out_ref in zip(sizes, out_refs):
                at = (d * heads + head) * HEAD_DIM
                out_ref[d] = q_ref[:, at:at + size * HEAD_DIM]
                head += size

    return pl.pallas_call(
        kernel,
        out_shape=[jax.ShapeDtypeStruct((devices, rows, n * HEAD_DIM), queries.dtype) for n in sizes],
        grid=(STEPS,),
        in_specs=[pl.BlockSpec((rows, width // STEPS), lambda i: (0, i))],
        out_specs=[pl.BlockSpec((some, rows, n * HEAD_DIM), lambda i: (i, 0, 0)) for n in sizes],
        cost_estimate=pl.CostEstimate(flops=16 * queries.size, bytes_accessed=4 * queries.size, transcendentals=0),
        name="pack_queries",
    )(queries)


def unpack_answers(answers):
    devices, rows, _ = answers[0].shape
    sizes = [x.shape[2] // HEAD_DIM for x in answers]
    heads = sum(sizes)
    some = devices // STEPS
    width = devices * heads * HEAD_DIM

    def kernel(*refs):
        out_ref = refs[-1]
        for d in range(some):
            head = 0
            for size, in_ref in zip(sizes, refs):
                at = (d * heads + head) * HEAD_DIM
                out_ref[:, at:at + size * HEAD_DIM] = in_ref[d]
                head += size

    return pl.pallas_call(
        kernel,
        out_shape=jax.ShapeDtypeStruct((rows, width), answers[0].dtype),
        grid=(STEPS,),
        in_specs=[pl.BlockSpec((some, rows, n * HEAD_DIM), lambda i: (i, 0, 0)) for n in sizes],
        out_specs=pl.BlockSpec((rows, width // STEPS), lambda i: (0, i)),
        name="unpack_answers",
    )(*answers)


def swapped(x, axis, bit):
    return lax.ppermute(x, axis, [(i, i ^ 1 << bit) for i in range(lax.axis_size(axis))])


def exchanged(x):
    return lax.all_to_all(x, "seq", split_axis=0, concat_axis=0, tiled=True)


def mask_table(first, heads, blocks, stretch, vertical, vert_count, slash, slash_count):
    lanes = -(-stretch // LANES) * LANES
    take = lambda x: lax.dynamic_slice_in_dim(x, first, heads, 0)
    verticals, live_vert, slashes, live_slash = take(vertical), take(vert_count), take(slash), take(slash_count)
    key_block = jnp.arange(blocks, dtype=jnp.int32)
    own = blocks - stretch + jnp.arange(lanes, dtype=jnp.int32)
    chosen = jnp.where(jnp.arange(verticals.shape[1]) < live_vert[:, None], verticals, -1)
    vert_hit = jnp.any(chosen[:, None, :] == key_block[None, :, None], axis=2)
    offset = jnp.where(jnp.arange(slashes.shape[1]) < live_slash[:, None], slashes + 1, 0)
    distance = own[None, :] - key_block[:, None]
    slash_hit = jnp.any(offset[:, :, None, None] == distance[None, None], axis=1)
    allowed = (distance == 0)[None] | ((distance > 0)[None] & (vert_hit[:, :, None] | slash_hit))
    return jnp.where(allowed, 0.0, HIDE).astype(jnp.float32)


def asked_sizes(heads):
    return (1, 1, heads - 2) if heads > 2 else (1,) * heads


def answer_sizes(heads):
    return (heads - 2, 1, 1) if heads > 2 else (1,) * heads


def body(queries, keys, values, vertical, vert_count, slash, slash_count):
    seq_count = lax.axis_size("seq")
    position = lax.axis_index("seq")
    query_rows = queries.shape[0]
    key_rows = keys.shape[0]
    sharers = seq_count // KV_HEADS
    heads = QUERY_HEADS // seq_count

    def shared(x):
        pieces = [x]
        for level in range(sharers.bit_length() - 1):
            pieces = pieces + [swapped(y, "seq", level) for y in pieces]
        return pieces

    own_keys = exchanged(pack_cache(keys, sharers))
    all_keys = shared(own_keys)
    own_values = exchanged(pack_cache(values, sharers))
    all_values = shared(own_values)
    packed = pack_queries(queries, seq_count, asked_sizes(heads))
    asked = []
    for size, part in zip(asked_sizes(heads), packed):
        part = exchanged(part).reshape(seq_count * query_rows, -1)
        asked += [(part, h) for h in range(size)]
    table = mask_table(
        position * heads, heads, seq_count * key_rows // BLOCK, seq_count * query_rows // BLOCK,
        vertical, vert_count, slash, slash_count,
    )
    side = (position % sharers).astype(jnp.int32).reshape(1)
    tables = [table[h][None] for h in range(heads)]
    answers = []
    head = 0
    for size in answer_sizes(heads):
        found = None
        for place in range(size):
            part, h = asked[head]
            found = attention(part, all_keys, all_values, tables[head], side, h, place, size, found)
            head += 1
        answers.append(exchanged(found.reshape(seq_count, query_rows, size * HEAD_DIM)))
    return unpack_answers(answers)


def solution(mesh):
    return jax.shard_map(
        body,
        mesh=mesh,
        in_specs=(
            P(("rep", "seq"), None),
            P(("rep", "seq"), None),
            P(("rep", "seq"), None),
            P("rep", None),
            P("rep"),
            P("rep", None),
            P("rep"),
        ),
        out_specs=P(("rep", "seq"), None),
        check_vma=False,
    )
```

profile of v0, /device:TPU:0, one launch (start us, length us, event | category | flops | bytes accessed | tf_op | source)
XLA Modules:
  0.0 309.3 jit_solution(12668244240844444649)
XLA Ops:
  0.0 3.8 %pack_queries.1 = (bf16[16,128,128]{2,1,0:T(8,128)(2,1)}, bf16[16,128,128]{2,1,0:T(8,128)(2,1)}, bf16[16,128,256]{2,1,0:T(8,128)(2,1)}) custom-call(bf16[128,8192]{1,0:T(8,128)(2,1)} %q_ref.1), custom_call_target="tpu_custom_call" | custom-call | flops 16777216 | bytes 4194304 | tf_op jit(solution)/shard_map/pack_queries/pallas_call | solution.py:198
  3.8 8.3 %all-to-all-start = ((bf16[16,128,128]{2,1,0:T(8,128)(2,1)}), bf16[16,128,128]{2,1,0:T(8,128)(2,1)S(1)}, u32[]{:S(2)}, u32[]{:S(2)}) async-start(bf16[16,128,128]{2,1,0:T(8,128)(2,1)} %get-tuple-element.8), calls=%async_computation | async-start | bytes 1048576 | tf_op jit(solution)/shard_map/all_to_all | solution.py:240
  12.2 3.4 %pack_cache.2 = bf16[16,256,128]{2,1,0:T(8,128)(2,1)} custom-call(bf16[512,1024]{1,0:T(8,128)(2,1)} %in_ref.2), custom_call_target="tpu_custom_call" | custom-call | flops 8388608 | bytes 2097152 | tf_op jit(solution)/shard_map/pack_cache/pallas_call | solution.py:174
  15.6 11.7 %all-to-all-done = bf16[16,128,128]{2,1,0:T(8,128)(2,1)S(1)} async-done(((bf16[16,128,128]{2,1,0:T(8,128)(2,1)}), bf16[16,128,128]{2,1,0:T(8,128)(2,1)S(1)}, u32[]{:S(2)}, u32[]{:S(2)}) %all-to-all-start) | async-done | bytes 524320 | tf_op jit(solution)/shard_map/all_to_all | solution.py:240
  27.2 0.0 copy-start.3
  27.2 0.8 copy-done.3
  28.0 3.9 %all-to-all-start.1 = ((bf16[16,256,128]{2,1,0:T(8,128)(2,1)}), bf16[16,256,128]{2,1,0:T(8,128)(2,1)S(1)}, u32[]{:S(2)}, u32[]{:S(2)}) async-start(bf16[16,256,128]{2,1,0:T(8,128)(2,1)} %pack_cache.2), calls=%async_computation.1 | async-start | bytes 2097152 | tf_op jit(solution)/shard_map/all_to_all | solution.py:240
  32.0 3.4 %pack_cache.3 = bf16[16,256,128]{2,1,0:T(8,128)(2,1)} custom-call(bf16[512,1024]{1,0:T(8,128)(2,1)} %in_ref.3), custom_call_target="tpu_custom_call" | custom-call | flops 8388608 | bytes 2097152 | tf_op jit(solution)/shard_map/pack_cache/pallas_call | solution.py:174
  35.5 0.0 copy-start.5
  35.5 0.0 copy-start.6
  35.5 0.0 copy-start.4
  35.5 20.2 %all-to-all-done.1.refs_0_ = bf16[16,256,128]{2,1,0:T(8,128)(2,1)S(1)} async-done(((bf16[16,256,128]{2,1,0:T(8,128)(2,1)}), bf16[16,256,128]{2,1,0:T(8,128)(2,1)S(1)}, u32[]{:S(2)}, u32[]{:S(2)}) %all-to-all-start.1) | async-done | bytes 1048608 | tf_op jit(solution)/shard_map/all_to_all | solution.py:240
  55.7 0.0 copy-start
  55.7 30.9 %all_to_all.40.refs_2_ = bf16[16,256,128]{2,1,0:T(8,128)(2,1)S(1)} all-to-all(bf16[16,256,128]{2,1,0:T(8,128)(2,1)} %pack_cache.3), channel_id=1, replica_groups=mesh['rep'=2,'seq'=16] {'seq'}, dimensions={0} | all-to-all | bytes 2097152 | tf_op jit(solution)/shard_map/all_to_all | solution.py:240
  86.5 0.0 copy-start.1
  86.5 3.9 %all-to-all-start.5 = ((bf16[16,128,256]{2,1,0:T(8,128)(2,1)}), bf16[16,128,256]{2,1,0:T(8,128)(2,1)S(1)}, u32[]{:S(2)}, u32[]{:S(2)}) async-start(bf16[16,128,256]{2,1,0:T(8,128)(2,1)} %get-tuple-element.10), calls=%async_computation.5 | async-start | bytes 2097152 | tf_op jit(solution)/shard_map/all_to_all | solution.py:240
  90.4 0.0 copy-done.5
  90.5 0.1 dynamic_slice.12
  90.5 0.0 copy-done.6
  90.5 0.1 dynamic_slice.14
  90.6 0.0 copy-done.4
  90.6 0.1 add_select_fusion
  90.7 2.0 collective-permute-start.1
  92.7 0.0 copy-done
  92.7 0.1 collective-permute-start
  92.8 0.8 dynamic-slice_select_fusion
  93.6 0.1 copy.10
  93.6 0.1 fusion
  93.8 1.7 compare_reduce_fusion
  95.5 0.1 or_select_fusion
  95.6 17.8 %all-to-all-done.5 = bf16[16,128,256]{2,1,0:T(8,128)(2,1)S(1)} async-done(((bf16[16,128,256]{2,1,0:T(8,128)(2,1)}), bf16[16,128,256]{2,1,0:T(8,128)(2,1)S(1)}, u32[]{:S(2)}, u32[]{:S(2)}) %all-to-all-start.5) | async-done | bytes 1048608 | tf_op jit(solution)/shard_map/all_to_all | solution.py:240
  113.4 6.2 %all-to-all-start.3 = ((bf16[16,128,128]{2,1,0:T(8,128)(2,1)}), bf16[16,128,128]{2,1,0:T(8,128)(2,1)}, u32[]{:S(2)}, u32[]{:S(2)}) async-start(bf16[16,128,128]{2,1,0:T(8,128)(2,1)} %get-tuple-element.9), calls=%async_computation.3 | async-start | bytes 1048576 | tf_op jit(solution)/shard_map/all_to_all | solution.py:240
  119.6 0.7 fusion.3
  120.4 0.0 copy-done.1
  120.4 11.1 %collective-permute-done.1.refs_3_ = bf16[16,256,128]{2,1,0:T(8,128)(2,1)} collective-permute-done((bf16[16,256,128]{2,1,0:T(8,128)(2,1)S(1)}, bf16[16,256,128]{2,1,0:T(8,128)(2,1)}, u32[]{:S(2)}, u32[]{:S(2)}) %collective-permute-start.1) | collective-permute-done | bytes 1048608 | tf_op jit(solution)/shard_map/ppermute | solution.py:236
  131.4 21.1 %collective-permute-done.refs_1_ = bf16[16,256,128]{2,1,0:T(8,128)(2,1)} collective-permute-done((bf16[16,256,128]{2,1,0:T(8,128)(2,1)S(1)}, bf16[16,256,128]{2,1,0:T(8,128)(2,1)}, u32[]{:S(2)}, u32[]{:S(2)}) %collective-permute-start) | collective-permute-done | bytes 1048608 | tf_op jit(solution)/shard_map/ppermute | solution.py:236
  152.5 0.0 copy-done.2
  152.5 27.4 %attention.7 = bf16[2048,128]{1,0:T(8,128)(2,1)} custom-call(s32[1]{0:T(128)} %bitcast.side_ref, f32[1,128,128]{2,1,0:T(8,128)} %get-tuple-element.11.table_ref, bf16[2048,256]{1,0:T(8,128)(2,1)} %bitcast.7, bf16[16,256,128]{2,1,0:T(8,128)(2,1)} %copy-done, bf16[16,256,128]{2,1,0:T(8,128)(2,1)} %collective-permute-done.refs_1_, ...), custom_call_target="tpu_custom_call" | custom-call | flops 8589934592 | bytes 5242880 | tf_op jit(solution)/shard_map/attention/pallas_call | solution.py:128
  179.9 0.0 all-to-all-done.3
  179.9 5.6 %all-to-all-start.7 = ((bf16[16,128,128]{2,1,0:T(8,128)(2,1)}), bf16[16,128,128]{2,1,0:T(8,128)(2,1)}, u32[]{:S(2)}, u32[]{:S(2)}) async-start(bf16[16,128,128]{2,1,0:T(8,128)(2,1)} %bitcast.12), calls=%async_computation.7 | async-start | bytes 1048576 | tf_op jit(solution)/shard_map/all_to_all | solution.py:240
  185.6 27.5 %attention.6 = bf16[2048,128]{1,0:T(8,128)(2,1)} custom-call(s32[1]{0:T(128)} %bitcast.side_ref, f32[1,128,128]{2,1,0:T(8,128)} %get-tuple-element.12.table_ref, bf16[2048,256]{1,0:T(8,128)(2,1)} %bitcast.8, bf16[16,256,128]{2,1,0:T(8,128)(2,1)} %copy-done, bf16[16,256,128]{2,1,0:T(8,128)(2,1)} %collective-permute-done.refs_1_, ...), custom_call_target="tpu_custom_call" | custom-call | flops 8589934592 | bytes 5242880 | tf_op jit(solution)/shard_map/attention/pallas_call | solution.py:128
  213.0 0.0 all-to-all-done.7.refs_2_
  213.1 6.9 %all-to-all-start.6 = ((bf16[16,128,128]{2,1,0:T(8,128)(2,1)}), bf16[16,128,128]{2,1,0:T(8,128)(2,1)}, u32[]{:S(2)}, u32[]{:S(2)}) async-start(bf16[16,128,128]{2,1,0:T(8,128)(2,1)} %bitcast.11), calls=%async_computation.6 | async-start | bytes 1048576 | tf_op jit(solution)/shard_map/all_to_all | solution.py:240
  220.0 27.5 %attention.4.refs_4_ = bf16[2048,256]{1,0:T(8,128)(2,1)} custom-call(s32[1]{0:T(128)} %bitcast.side_ref, f32[1,128,128]{2,1,0:T(8,128)} %get-tuple-element.13.table_ref, bf16[2048,128]{1,0:T(8,128)(2,1)} %bitcast.2.q_ref, bf16[16,256,128]{2,1,0:T(8,128)(2,1)} %copy-done, bf16[16,256,128]{2,1,0:T(8,128)(2,1)} %collective-permute-done.refs_1_, ...), custom_call_target="tpu_custom_call" | custom-call | flops 8589934592 | bytes 5242880 | tf_op jit(solution)/shard_map/attention/pallas_call | solution.py:128
  247.5 27.5 %attention.5 = bf16[2048,256]{1,0:T(8,128)(2,1)} custom-call(s32[1]{0:T(128)} %bitcast.side_ref, f32[1,128,128]{2,1,0:T(8,128)} %get-tuple-element.14.table_ref, bf16[2048,128]{1,0:T(8,128)(2,1)} %bitcast.10, bf16[16,256,128]{2,1,0:T(8,128)(2,1)} %copy-done, bf16[16,256,128]{2,1,0:T(8,128)(2,1)} %collective-permute-done.refs_1_, ...), custom_call_target="tpu_custom_call", output_to_operand_aliasing={{}: (7, {})} | custom-call | flops 8589934592 | bytes 5242880 | tf_op jit(solution)/shard_map/attention/pallas_call | solution.py:128
  274.9 0.0 all-to-all-done.6.refs_1_
  274.9 30.4 %all_to_all.41.refs_0_ = bf16[16,128,256]{2,1,0:T(8,128)(2,1)} all-to-all(bf16[16,128,256]{2,1,0:T(8,128)(2,1)} %bitcast.9), channel_id=1, replica_groups=mesh['rep'=2,'seq'=16] {'seq'}, dimensions={0} | all-to-all | bytes 2097152 | tf_op jit(solution)/shard_map/all_to_all | solution.py:240
  305.4 3.9 %unpack_answers.1 = bf16[128,8192]{1,0:T(8,128)(2,1)} custom-call(bf16[16,128,256]{2,1,0:T(8,128)(2,1)} %all_to_all.41.refs_0_, bf16[16,128,128]{2,1,0:T(8,128)(2,1)} %all-to-all-done.6.refs_1_, bf16[16,128,128]{2,1,0:T(8,128)(2,1)} %all-to-all-done.7.refs_2_), custom_call_target="tpu_custom_call" | custom-call | tf_op jit(solution)/shard_map/unpack_answers/pallas_call | solution.py:225
  (4 shorter events, 0.0 us)
Async XLA Ops:
  3.8 23.4 %all-to-all-start = ((bf16[16,128,128]{2,1,0:T(8,128)(2,1)}), bf16[16,128,128]{2,1,0:T(8,128)(2,1)S(1)}, u32[]{:S(2)}, u32[]{:S(2)}) async-start(bf16[16,128,128]{2,1,0:T(8,128)(2,1)} %get-tuple-element.8), calls=%async_computation | async-start | bytes 1048576 | tf_op jit(solution)/shard_map/all_to_all | solution.py:240
  27.2 0.8 copy-start.3
  28.0 27.6 %all-to-all-start.1 = ((bf16[16,256,128]{2,1,0:T(8,128)(2,1)}), bf16[16,256,128]{2,1,0:T(8,128)(2,1)S(1)}, u32[]{:S(2)}, u32[]{:S(2)}) async-start(bf16[16,256,128]{2,1,0:T(8,128)(2,1)} %pack_cache.2), calls=%async_computation.1 | async-start | bytes 2097152 | tf_op jit(solution)/shard_map/all_to_all | solution.py:240
  35.5 55.0 %copy-start.5 = (s32[64]{0:T(128)S(1)}, s32[64]{0:T(128)}, u32[]{:S(2)}) copy-start(s32[64]{0:T(128)} %param.11) | copy-start | bytes 772
  35.5 55.1 %copy-start.6 = (s32[64]{0:T(128)S(1)}, s32[64]{0:T(128)}, u32[]{:S(2)}) copy-start(s32[64]{0:T(128)} %param.13) | copy-start | bytes 772
  35.5 55.2 %copy-start.4 = (s32[64,32]{0,1:T(8,128)S(1)}, s32[64,32]{0,1:T(8,128)}, u32[]{:S(2)}) copy-start(s32[64,32]{0,1:T(8,128)} %param.12) | copy-start | bytes 24580
  55.7 37.0 %copy-start = (bf16[16,256,128]{2,1,0:T(8,128)(2,1)}, bf16[16,256,128]{2,1,0:T(8,128)(2,1)S(1)}, u32[]{:S(2)}) copy-start(bf16[16,256,128]{2,1,0:T(8,128)(2,1)S(1)} %all-to-all-done.1.refs_0_) | copy-start | bytes 3145732
  86.5 33.8 %copy-start.1 = (bf16[16,256,128]{2,1,0:T(8,128)(2,1)}, bf16[16,256,128]{2,1,0:T(8,128)(2,1)S(1)}, u32[]{:S(2)}) copy-start(bf16[16,256,128]{2,1,0:T(8,128)(2,1)S(1)} %all_to_all.40.refs_2_) | copy-start | bytes 3145732
  86.5 26.9 %all-to-all-start.5 = ((bf16[16,128,256]{2,1,0:T(8,128)(2,1)}), bf16[16,128,256]{2,1,0:T(8,128)(2,1)S(1)}, u32[]{:S(2)}, u32[]{:S(2)}) async-start(bf16[16,128,256]{2,1,0:T(8,128)(2,1)} %get-tuple-element.10), calls=%async_computation.5 | async-start | bytes 2097152 | tf_op jit(solution)/shard_map/all_to_all | solution.py:240
  90.7 40.7 %collective-permute-start.1 = (bf16[16,256,128]{2,1,0:T(8,128)(2,1)S(1)}, bf16[16,256,128]{2,1,0:T(8,128)(2,1)}, u32[]{:S(2)}, u32[]{:S(2)}) collective-permute-start(bf16[16,256,128]{2,1,0:T(8,128)(2,1)S(1)} %all_to_all.40.refs_2_), channel_id=1, source_target_pairs={{0,1},{1,0},{2,3},{3,2},{4,5},{5,4},{6,7},{7,6},{8,9},{9,8},{10,11... | collective-permute-start | bytes 3145736 | tf_op jit(solution)/shard_map/ppermute | solution.py:236
  92.7 59.8 %collective-permute-start = (bf16[16,256,128]{2,1,0:T(8,128)(2,1)S(1)}, bf16[16,256,128]{2,1,0:T(8,128)(2,1)}, u32[]{:S(2)}, u32[]{:S(2)}) collective-permute-start(bf16[16,256,128]{2,1,0:T(8,128)(2,1)S(1)} %all-to-all-done.1.refs_0_), channel_id=1, source_target_pairs={{0,1},{1,0},{2,3},{3,2},{4,5},{5,4},{6,7},{7,6},{8,9},{9,8},{10,11... | collective-permute-start | bytes 3145736 | tf_op jit(solution)/shard_map/ppermute | solution.py:236
  113.4 39.1 %copy-start.2 = (bf16[16,128,256]{2,1,0:T(8,128)(2,1)}, bf16[16,128,256]{2,1,0:T(8,128)(2,1)S(1)}, u32[]{:S(2)}) copy-start(bf16[16,128,256]{2,1,0:T(8,128)(2,1)S(1)} %all-to-all-done.5) | copy-start | bytes 3145732
  113.4 66.5 %all-to-all-start.3 = ((bf16[16,128,128]{2,1,0:T(8,128)(2,1)}), bf16[16,128,128]{2,1,0:T(8,128)(2,1)}, u32[]{:S(2)}, u32[]{:S(2)}) async-start(bf16[16,128,128]{2,1,0:T(8,128)(2,1)} %get-tuple-element.9), calls=%async_computation.3 | async-start | bytes 1048576 | tf_op jit(solution)/shard_map/all_to_all | solution.py:240
  179.9 33.1 %all-to-all-start.7 = ((bf16[16,128,128]{2,1,0:T(8,128)(2,1)}), bf16[16,128,128]{2,1,0:T(8,128)(2,1)}, u32[]{:S(2)}, u32[]{:S(2)}) async-start(bf16[16,128,128]{2,1,0:T(8,128)(2,1)} %bitcast.12), calls=%async_computation.7 | async-start | bytes 1048576 | tf_op jit(solution)/shard_map/all_to_all | solution.py:240
  213.1 61.9 %all-to-all-start.6 = ((bf16[16,128,128]{2,1,0:T(8,128)(2,1)}), bf16[16,128,128]{2,1,0:T(8,128)(2,1)}, u32[]{:S(2)}, u32[]{:S(2)}) async-start(bf16[16,128,128]{2,1,0:T(8,128)(2,1)} %bitcast.11), calls=%async_computation.6 | async-start | bytes 1048576 | tf_op jit(solution)/shard_map/all_to_all | solution.py:240
where the time goes:
time: 311 us; the launch traced here: 309 us
  Pallas kernels  124 us (40%)
  waiting for transfers between devices  81.8 us (26%)
  blocking collectives  61.3 us (20%)
  starting transfers between devices  37 us (12%)
    pallas_call x4, Pallas kernels, attention(): pl.pallas_call(functools.partial(attention_kernel, factor, pieces), out_s...  110 us
    all_to_all x2, blocking collectives, exchanged(): return lax.all_to_all(x, 'seq', split_axis=0, concat_axis=0, tiled=True)  61.3 us
    all_to_all x6, waiting for transfers between devices, exchanged(): return lax.all_to_all(x, 'seq', split_axis=0, concat_axis=0, tiled=True)  49.7 us
    all_to_all x6, starting transfers between devices, exchanged(): return lax.all_to_all(x, 'seq', split_axis=0, concat_axis=0, tiled=True)  34.9 us
    ppermute x2, waiting for transfers between devices, swapped(): lax.ppermute(x, axis, [(i, i ^ 1 << bit) for i in range(lax.axis_size(axi...  32.1 us
    pallas_call x2, Pallas kernels, pack_cache(): pl.pallas_call(kernel, out_shape=jax.ShapeDtypeStruct((KV_HEADS * sharers...  6.88 us
  transfers between devices with their start and end apart: 8, of which 5 were waited for; matrix products, arithmetic and copies ran while one was open for 1% of the time, Pallas kernels for 38%

commit v1 on v0

v1 whole, which is shorter than its diff:
```python
import functools
import math

import jax
import jax.numpy as jnp
from jax import lax
from jax.experimental import pallas as pl
from jax.experimental.pallas import tpu as pltpu
from jax.sharding import PartitionSpec as P


QUERY_HEADS = 64
KV_HEADS = 8
HEAD_DIM = 128
BLOCK = 64
LANES = 128
ONES = 16
HIDE = -1e30
STEPS = 4
SPAN = 4
GROUP = 8


def attention_kernel(factor, pieces, first, place, steps_ref, list_ref, table_hbm, q_hbm, *refs):
    cache_refs, out_hbm, scratch = refs[:2 * pieces], refs[-13], refs[-12:]
    keys, values, table, q, out, qa, s_even, s_odd, acc, fetch_sem, out_sem, cache_sem = scratch
    width = HEAD_DIM
    rows = SPAN * BLOCK
    chunk = GROUP * BLOCK
    lanes = table.shape[1]
    blocks = keys.shape[0] // BLOCK - 1
    tiles = q.shape[0] // rows
    length = list_ref.shape[0] // tiles
    piece_size = blocks * BLOCK // pieces
    both = range(2)

    fetches = [
        pltpu.make_async_copy(table_hbm, table, fetch_sem.at[0]),
        pltpu.make_async_copy(q_hbm.at[:, first * width:(first + 1) * width], q, fetch_sem.at[1]),
    ]
    loads = []
    for n, (home, cached) in enumerate(((keys, cache_refs[:pieces]), (values, cache_refs[pieces:]))):
        for p in range(pieces):
            loads.append(
                pltpu.make_async_copy(cached[p], home.at[pl.ds(p * piece_size, piece_size)], cache_sem.at[n * pieces + p])
            )
    for copy in fetches + loads:
        copy.start()
    for home in (keys, values):
        home[blocks * BLOCK:, :] = jnp.zeros((BLOCK, width), home.dtype)
    for copy in fetches:
        copy.wait()

    def prepare(tile, carry):
        qa[tile, :width, :] = q[pl.ds(pl.multiple_of(tile * rows, rows), rows), :].T
        column_block = lax.broadcasted_iota(jnp.int32, (lanes, rows), 1) // BLOCK + tile * SPAN
        chosen = lax.broadcasted_iota(jnp.int32, (lanes, rows), 0) == column_block
        qa[tile, width:, :] = chosen.astype(jnp.float32).astype(jnp.bfloat16)
        return carry

    lax.fori_loop(0, tiles, prepare, 0)
    for copy in loads:
        copy.wait()

    def sent(couple):
        where = pl.ds(pl.multiple_of(couple * 2 * rows, 2 * rows), 2 * rows)
        return pltpu.make_async_copy(out.at[where], out_hbm.at[where, place * width:(place + 1) * width], out_sem.at[couple])

    def serve(couple, carry):
        def entries(x, step):
            at = (couple * 2 + x) * length + step * GROUP
            return [list_ref[at + b] for b in range(GROUP)]

        def gathered(home, x, step):
            return jnp.concatenate(
                [home[pl.ds(pl.multiple_of(e * BLOCK, BLOCK), BLOCK), :] for e in entries(x, step)], axis=0
            )

        def product(x, step):
            bias = jnp.concatenate(
                [
                    jnp.broadcast_to(table[pl.ds(e, 1), :], (BLOCK, lanes)).astype(jnp.bfloat16)
                    for e in entries(x, step)
                ],
                axis=0,
            )
            left = jnp.concatenate([gathered(keys, x, step), bias], axis=1)
            return jnp.dot(left, qa[couple * 2 + x], preferred_element_type=jnp.float32)

        def top_of(s):
            return jnp.max(s.reshape(chunk // 8, 8, rows), axis=0)

        def score(step, s_ref):
            tops = []
            for x in both:
                s = product(x, step)
                s_ref[x] = s
                tops.append(top_of(s))
            return tuple(tops)

        def fold(step, s_ref, peaks, parts):
            news = []
            for x in both:
                top = jnp.maximum(peaks[x], jnp.max(parts[x], axis=0, keepdims=True))
                alpha = jnp.exp2((peaks[x] - top) * factor)
                p = jnp.exp2((s_ref[x] - top) * factor).astype(jnp.bfloat16)
                held = gathered(values, x, step).T
                held = jnp.concatenate([held, jnp.ones((ONES, chunk), jnp.bfloat16)], axis=0)
                acc[x] = acc[x] * alpha + jnp.dot(held, p, preferred_element_type=jnp.float32)
                news.append(top)
            return tuple(news)

        acc[...] = jnp.zeros_like(acc)
        parts = []
        for x in both:
            s = product(x, 0)
            row = lax.broadcasted_iota(jnp.int32, s.shape, 0)
            column = lax.broadcasted_iota(jnp.int32, s.shape, 1)
            s = jnp.where((row <= column) | (row >= rows), s, HIDE)
            s_even[x] = s
            parts.append(top_of(s))
        peaks = (jnp.full((1, rows), HIDE, jnp.float32),) * 2
        count = jnp.maximum(steps_ref[couple * 2], steps_ref[couple * 2 + 1])

        def pair(i, carry):
            peaks, parts = carry
            parts_odd = score(2 * i + 1, s_odd)
            peaks = fold(2 * i, s_even, peaks, parts)
            parts = score(2 * i + 2, s_even)
            peaks = fold(2 * i + 1, s_odd, peaks, parts_odd)
            return peaks, parts

        peaks, parts = lax.fori_loop(0, count // 2, pair, (peaks, tuple(parts)))

        @pl.when(count % 2 == 1)
        def _():
            fold(count - 1, s_even, peaks, parts)

        for x in both:
            answer = acc[x, :width, :] / acc[x, width:width + 1, :]
            at = pl.multiple_of((couple * 2 + x) * rows, rows)
            out[pl.ds(at, rows), :] = answer.T.astype(out.dtype)
        sent(couple).start()
        return carry

    lax.fori_loop(0, tiles // 2, serve, 0)

    def drain(couple, carry):
        sent(couple).wait()
        return carry

    lax.fori_loop(0, tiles // 2, drain, 0)


def attention(q, keys, values, table, entries, steps, first=0, place=0, breadth=1, prior=None):
    pieces = len(keys)
    keys, values = [[x.reshape(-1, HEAD_DIM) for x in some] for some in (keys, values)]
    context = pieces * keys[0].shape[0]
    lanes = table.shape[1]
    rows = SPAN * BLOCK
    chunk = GROUP * BLOCK
    tiles = q.shape[0] // rows
    factor = math.log2(math.e) / math.sqrt(HEAD_DIM)
    pairs = q.shape[0] * context
    priors = [] if prior is None else [prior]
    anywhere = pl.BlockSpec(memory_space=pl.ANY)
    scalars = pl.BlockSpec(memory_space=pltpu.SMEM)
    return pl.pallas_call(
        functools.partial(attention_kernel, factor, pieces, first, place),
        out_shape=jax.ShapeDtypeStruct((q.shape[0], breadth * HEAD_DIM), jnp.bfloat16),
        in_specs=[scalars, scalars] + [anywhere] * (2 + 2 * pieces + len(priors)),
        out_specs=anywhere,
        scratch_shapes=[
            pltpu.VMEM((context + BLOCK, HEAD_DIM), jnp.bfloat16),
            pltpu.VMEM((context + BLOCK, HEAD_DIM), jnp.bfloat16),
            pltpu.VMEM(table.shape, jnp.float32),
            pltpu.VMEM((q.shape[0], HEAD_DIM), jnp.bfloat16),
            pltpu.VMEM((q.shape[0], HEAD_DIM), jnp.bfloat16),
            pltpu.VMEM((tiles, HEAD_DIM + lanes, rows), jnp.bfloat16),
            pltpu.VMEM((2, chunk, rows), jnp.float32),
            pltpu.VMEM((2, chunk, rows), jnp.float32),
            pltpu.VMEM((2, HEAD_DIM + ONES, rows), jnp.float32),
            pltpu.SemaphoreType.DMA((2,)),
            pltpu.SemaphoreType.DMA((tiles // 2,)),
            pltpu.SemaphoreType.DMA((2 * pieces,)),
        ],
        compiler_params=pltpu.CompilerParams(vmem_limit_bytes=67000000),
        cost_estimate=pl.CostEstimate(
            flops=4 * pairs * HEAD_DIM,
            bytes_accessed=4 * q.shape[0] * HEAD_DIM + 4 * pieces * keys[0].size,
            transcendentals=pairs,
        ),
        input_output_aliases={4 + 2 * pieces: 0} if priors else {},
        name="attention",
    )(steps, entries, table, q, *keys, *values, *priors)


def make_plan(natural, where_is, heads_at, heads, stretch, vertical, vert_count, slash, slash_count):
    blocks = natural.shape[0]
    lanes = -(-stretch // LANES) * LANES
    tiles = stretch // SPAN
    take = lambda x: lax.dynamic_slice_in_dim(x, heads_at, heads, 0)
    verticals, live_vert, slashes, live_slash = take(vertical), take(vert_count), take(slash), take(slash_count)
    lane = jnp.arange(lanes, dtype=jnp.int32)
    tile = jnp.arange(tiles, dtype=jnp.int32)
    index = jnp.arange(blocks, dtype=jnp.int32)
    distance = blocks - stretch + lane[None, :] - natural[:, None]
    chosen = jnp.where(jnp.arange(verticals.shape[1]) < live_vert[:, None], verticals, -1)
    vert_hit = jnp.any(chosen[:, None, :] == natural[None, :, None], axis=2)
    offset = jnp.where(jnp.arange(slashes.shape[1]) < live_slash[:, None], slashes + 1, 0)
    slash_hit = jnp.any(offset[:, :, None, None] == distance[None, None], axis=1)
    allowed = (distance == 0)[None] | ((distance > 0)[None] & (vert_hit[:, :, None] | slash_hit))
    table = jnp.where(allowed, 0.0, HIDE).astype(jnp.float32)
    table = jnp.pad(table, ((0, 0), (0, 8), (0, 0)), constant_values=HIDE)

    member = (lane[None, :] // SPAN == tile[:, None]).astype(jnp.bfloat16)
    hits = jnp.einsum("hjl,tl->htj", allowed.astype(jnp.bfloat16), member, preferred_element_type=jnp.float32)
    own = blocks - stretch + tile * SPAN
    needed = (hits > 0) & (natural[None, None, :] < own[None, :, None])
    before = (index[:, None] < index[None, :]).astype(jnp.bfloat16)
    rank = jnp.einsum("htj,jk->htk", needed.astype(jnp.bfloat16), before, preferred_element_type=jnp.float32)
    rank = jnp.where(needed, rank.astype(jnp.int32) + SPAN, -1)
    spot = jnp.arange(blocks + 2 * GROUP, dtype=jnp.int32)
    hit = rank[:, :, None, :] == spot[None, None, :, None]
    entries = jnp.min(jnp.where(hit, index[None, None, None, :], blocks), axis=3)
    mine = where_is(jnp.minimum(own[:, None] + spot[None, :], blocks - 1))
    entries = jnp.where(spot < SPAN, mine[None], entries)
    steps = (jnp.sum(needed, axis=2, dtype=jnp.int32) + SPAN + GROUP - 1) // GROUP
    return table, entries.astype(jnp.int32), steps.astype(jnp.int32)


def traded(index):
    return index & ~3 | (index & 1) << 1 | (index >> 1) & 1


def seat(index, flip):
    return jnp.where(flip == 1, traded(index), index)


def pack_cache(x, sharers, flip):
    rows, _ = x.shape
    piece_rows = rows // sharers
    some = KV_HEADS // STEPS

    def kernel(flip_ref, in_ref, out_ref):
        for g in range(some):
            for p in range(sharers):
                out_ref[seat(g * sharers + p, flip_ref[0])] = in_ref[p * piece_rows:(p + 1) * piece_rows, g * HEAD_DIM:(g + 1) * HEAD_DIM]

    return pl.pallas_call(
        kernel,
        out_shape=jax.ShapeDtypeStruct((KV_HEADS * sharers, piece_rows, HEAD_DIM), x.dtype),
        grid_spec=pltpu.PrefetchScalarGridSpec(
            num_scalar_prefetch=1,
            grid=(STEPS,),
            in_specs=[pl.BlockSpec((rows, some * HEAD_DIM), lambda i, s: (0, i))],
            out_specs=pl.BlockSpec((some * sharers, piece_rows, HEAD_DIM), lambda i, s: (i, 0, 0)),
        ),
        cost_estimate=pl.CostEstimate(flops=16 * x.size, bytes_accessed=4 * x.size, transcendentals=0),
        name="pack_cache",
    )(flip, x)


def pack_queries(queries, devices, sizes, flip):
    rows, width = queries.shape
    heads = sum(sizes)
    some = devices // STEPS

    def kernel(flip_ref, q_ref, *out_refs):
        for d in range(some):
            head = 0
            for size, out_ref in zip(sizes, out_refs):
                at = (d * heads + head) * HEAD_DIM
                out_ref[seat(d, flip_ref[0])] = q_ref[:, at:at + size * HEAD_DIM]
                head += size

    return pl.pallas_call(
        kernel,
        out_shape=[jax.ShapeDtypeStruct((devices, rows, n * HEAD_DIM), queries.dtype) for n in sizes],
        grid_spec=pltpu.PrefetchScalarGridSpec(
            num_scalar_prefetch=1,
            grid=(STEPS,),
            in_specs=[pl.BlockSpec((rows, width // STEPS), lambda i, s: (0, i))],
            out_specs=[pl.BlockSpec((some, rows, n * HEAD_DIM), lambda i, s: (i, 0, 0)) for n in sizes],
        ),
        cost_estimate=pl.CostEstimate(flops=16 * queries.size, bytes_accessed=4 * queries.size, transcendentals=0),
        name="pack_queries",
    )(flip, queries)


def unpack_answers(answers, flip):
    devices, rows, _ = answers[0].shape
    sizes = [x.shape[2] // HEAD_DIM for x in answers]
    heads = sum(sizes)
    some = devices // STEPS
    width = devices * heads * HEAD_DIM

    def kernel(flip_ref, *refs):
        out_ref = refs[-1]
        for d in range(some):
            head = 0
            for size, in_ref in zip(sizes, refs):
                at = (d * heads + head) * HEAD_DIM
                out_ref[:, at:at + size * HEAD_DIM] = in_ref[seat(d, flip_ref[0])]
                head += size

    return pl.pallas_call(
        kernel,
        out_shape=jax.ShapeDtypeStruct((rows, width), answers[0].dtype),
        grid_spec=pltpu.PrefetchScalarGridSpec(
            num_scalar_prefetch=1,
            grid=(STEPS,),
            in_specs=[pl.BlockSpec((some, rows, n * HEAD_DIM), lambda i, s: (i, 0, 0)) for n in sizes],
            out_specs=pl.BlockSpec((rows, width // STEPS), lambda i, s: (0, i)),
        ),
        name="unpack_answers",
    )(flip, *answers)


def swapped(x, bit):
    count = lax.axis_size("seq")
    moves = []
    for rep in range(lax.axis_size("rep")):
        turn = traded if rep % 2 else int
        moves += [(rep * count + i, rep * count + turn(turn(i) ^ 1 << bit)) for i in range(count)]
    return lax.ppermute(x, ("rep", "seq"), moves)


def exchanged(x):
    return lax.all_to_all(x, "seq", split_axis=0, concat_axis=0, tiled=True)


def asked_sizes(heads):
    return (1, 1, heads - 2) if heads > 2 else (1,) * heads


def answer_sizes(heads):
    return (heads - 2, 1, 1) if heads > 2 else (1,) * heads


def body(queries, keys, values, vertical, vert_count, slash, slash_count):
    seq_count = lax.axis_size("seq")
    flip = (lax.axis_index("rep") % 2).astype(jnp.int32).reshape(1)
    position = seat(lax.axis_index("seq"), flip[0])
    query_rows = queries.shape[0]
    key_rows = keys.shape[0]
    sharers = seq_count // KV_HEADS
    heads = QUERY_HEADS // seq_count

    def shared(x):
        pieces = [x]
        for level in range(sharers.bit_length() - 1):
            pieces = pieces + [swapped(y, level) for y in pieces]
        return pieces

    own_keys = exchanged(pack_cache(keys, sharers, flip))
    all_keys = shared(own_keys)
    own_values = exchanged(pack_cache(values, sharers, flip))
    all_values = shared(own_values)
    packed = pack_queries(queries, seq_count, asked_sizes(heads), flip)
    asked = []
    for size, part in zip(asked_sizes(heads), packed):
        part = exchanged(part).reshape(seq_count * query_rows, -1)
        asked += [(part, h) for h in range(size)]
    piece_blocks = key_rows // sharers // BLOCK
    side = position % sharers
    spot = jnp.arange(seq_count * key_rows // BLOCK, dtype=jnp.int32)
    piece = spot // (seq_count * piece_blocks)
    sender = spot // piece_blocks % seq_count
    natural = (sender * sharers + (piece ^ side)) * piece_blocks + spot % piece_blocks

    def where_is(block):
        piece = block // piece_blocks % sharers ^ side
        return (piece * seq_count + block // (piece_blocks * sharers)) * piece_blocks + block % piece_blocks

    table, entries, steps = make_plan(
        natural, where_is, position * heads, heads, seq_count * query_rows // BLOCK,
        vertical, vert_count, slash, slash_count,
    )
    plans = [(table[h], entries[h].reshape(-1), steps[h]) for h in range(heads)]
    answers = []
    head = 0
    for size in answer_sizes(heads):
        found = None
        for place in range(size):
            part, h = asked[head]
            found = attention(part, all_keys, all_values, *plans[head], h, place, size, found)
            head += 1
        answers.append(exchanged(found.reshape(seq_count, query_rows, size * HEAD_DIM)))
    return unpack_answers(answers, flip)


def solution(mesh):
    return jax.shard_map(
        body,
        mesh=mesh,
        in_specs=(
            P(("rep", "seq"), None),
            P(("rep", "seq"), None),
            P(("rep", "seq"), None),
            P("rep", None),
            P("rep"),
            P("rep", None),
            P("rep"),
        ),
        out_specs=P(("rep", "seq"), None),
        check_vma=False,
    )
```

time: 311 us -> 276 us (0.89)
  blocking collectives: 61.3 us -> 29.7 us
  Pallas kernels: 124 us -> 101 us
  starting transfers between devices: 37 us -> 53.2 us
  local copies, waits for them, and re-layouts: 1.8 us -> 5.11 us
    all_to_all x2 -> x1, blocking collectives: 61.3 us -> 29.7 us  [exchanged(): return lax.all_to_all(x, 'seq', split_axis=0, concat_axis=0, tiled=True)]
    pallas_call x4, Pallas kernels: 110 us -> 86.7 us  [attention(): pl.pallas_call(functools.partial(attention_kernel, factor, pieces, first,...]
    ppermute x2, waiting for transfers between devices: 32.1 us -> 10.9 us  [swapped(): return lax.ppermute(x, ('rep', 'seq'), moves)]
    all_to_all x6 -> x7, waiting for transfers between devices: 49.7 us -> 69 us  [exchanged(): return lax.all_to_all(x, 'seq', split_axis=0, concat_axis=0, tiled=True)]
    all_to_all x6 -> x7, starting transfers between devices: 34.9 us -> 51.1 us  [exchanged(): return lax.all_to_all(x, 'seq', split_axis=0, concat_axis=0, tiled=True)]
  transfers between devices with their start and end apart: 8 -> 9, of which waited for: 5 -> 5; matrix products, arithmetic and copies ran while one was open for 1% -> 3% of each run, Pallas kernels for 38% -> 34%
where the time goes in v1:
time: 276 us; the launch traced here: 274 us
  Pallas kernels  101 us (37%)
  waiting for transfers between devices  79.9 us (29%)
  starting transfers between devices  53.2 us (19%)
  blocking collectives  29.7 us (11%)
  local copies, waits for them, and re-layouts  5.11 us (2%)
  other arithmetic  4.32 us (2%)
    pallas_call x4, Pallas kernels, attention(): pl.pallas_call(functools.partial(attention_kernel, factor, pieces, first,...  86.7 us
    all_to_all x7, waiting for transfers between devices, exchanged(): return lax.all_to_all(x, 'seq', split_axis=0, concat_axis=0, tiled=True)  69 us
    all_to_all x7, starting transfers between devices, exchanged(): return lax.all_to_all(x, 'seq', split_axis=0, concat_axis=0, tiled=True)  51.1 us
    all_to_all x1, blocking collectives, exchanged(): return lax.all_to_all(x, 'seq', split_axis=0, concat_axis=0, tiled=True)  29.7 us
    ppermute x2, waiting for transfers between devices, swapped(): return lax.ppermute(x, ('rep', 'seq'), moves)  10.9 us
    pallas_call x2, Pallas kernels, pack_cache(): pl.pallas_call(kernel, out_shape=jax.ShapeDtypeStruct((KV_HEADS * sharers...  6.89 us
  transfers between devices with their start and end apart: 9, of which 5 were waited for; matrix products, arithmetic and copies ran while one was open for 3% of the time, Pallas kernels for 34%

profile of v1, /device:TPU:0, one launch (start us, length us, event | category | flops | bytes accessed | tf_op | source)
XLA Modules:
  0.0 274.3 jit_solution(6020453804551868431)
XLA Ops:
  0.0 3.8 %pack_queries.1 = (bf16[16,128,128]{2,1,0:T(8,128)(2,1)}, bf16[16,128,128]{2,1,0:T(8,128)(2,1)}, bf16[16,128,256]{2,1,0:T(8,128)(2,1)}) custom-call(s32[1]{0:T(128)} %bitcast.flip_ref, bf16[128,8192]{1,0:T(8,128)(2,1)} %q_ref.1), custom_call_target="tpu_custom_call" | custom-call | flops 16777216 | bytes 4194304 | tf_op jit(solution)/shard_map/pack_queries/pallas_call | solution.py:277
  3.8 8.3 %all-to-all-start = ((bf16[16,128,128]{2,1,0:T(8,128)(2,1)}), bf16[16,128,128]{2,1,0:T(8,128)(2,1)S(1)}, u32[]{:S(2)}, u32[]{:S(2)}) async-start(bf16[16,128,128]{2,1,0:T(8,128)(2,1)} %get-tuple-element.8), calls=%async_computation | async-start | bytes 1048576 | tf_op jit(solution)/shard_map/all_to_all | solution.py:330
  12.2 3.4 %pack_cache.2 = bf16[16,256,128]{2,1,0:T(8,128)(2,1)} custom-call(s32[1]{0:T(128)} %bitcast.flip_ref, bf16[512,1024]{1,0:T(8,128)(2,1)} %in_ref.2), custom_call_target="tpu_custom_call" | custom-call | flops 8388608 | bytes 2097152 | tf_op jit(solution)/shard_map/pack_cache/pallas_call | solution.py:250
  15.6 11.6 %all-to-all-done = bf16[16,128,128]{2,1,0:T(8,128)(2,1)S(1)} async-done(((bf16[16,128,128]{2,1,0:T(8,128)(2,1)}), bf16[16,128,128]{2,1,0:T(8,128)(2,1)S(1)}, u32[]{:S(2)}, u32[]{:S(2)}) %all-to-all-start) | async-done | bytes 524320 | tf_op jit(solution)/shard_map/all_to_all | solution.py:330
  27.3 0.8 copy-done.3
  28.1 3.9 %all-to-all-start.1 = ((bf16[16,256,128]{2,1,0:T(8,128)(2,1)}), bf16[16,256,128]{2,1,0:T(8,128)(2,1)S(1)}, u32[]{:S(2)}, u32[]{:S(2)}) async-start(bf16[16,256,128]{2,1,0:T(8,128)(2,1)} %pack_cache.2), calls=%async_computation.1 | async-start | bytes 2097152 | tf_op jit(solution)/shard_map/all_to_all | solution.py:330
  32.0 0.0 copy-start.5
  32.0 0.0 copy-start.6
  32.0 0.0 copy-start.4
  32.0 3.5 %pack_cache.3 = bf16[16,256,128]{2,1,0:T(8,128)(2,1)} custom-call(s32[1]{0:T(128)} %bitcast.flip_ref, bf16[512,1024]{1,0:T(8,128)(2,1)} %in_ref.3), custom_call_target="tpu_custom_call" | custom-call | flops 8388608 | bytes 2097152 | tf_op jit(solution)/shard_map/pack_cache/pallas_call | solution.py:250
  35.5 20.2 %all-to-all-done.1 = bf16[16,256,128]{2,1,0:T(8,128)(2,1)S(1)} async-done(((bf16[16,256,128]{2,1,0:T(8,128)(2,1)}), bf16[16,256,128]{2,1,0:T(8,128)(2,1)S(1)}, u32[]{:S(2)}, u32[]{:S(2)}) %all-to-all-start.1) | async-done | bytes 1048608 | tf_op jit(solution)/shard_map/all_to_all | solution.py:330
  55.7 5.9 %all-to-all-start.2 = ((bf16[16,256,128]{2,1,0:T(8,128)(2,1)}), bf16[16,256,128]{2,1,0:T(8,128)(2,1)S(1)}, u32[]{:S(2)}, u32[]{:S(2)}) async-start(bf16[16,256,128]{2,1,0:T(8,128)(2,1)} %pack_cache.3), calls=%async_computation.2 | async-start | bytes 2097152 | tf_op jit(solution)/shard_map/all_to_all | solution.py:330
  61.6 0.1 dynamic_slice.12
  61.7 0.1 dynamic_slice.14
  61.8 0.1 add_select_fusion
  61.8 0.1 copy.10
  61.9 0.8 dynamic-slice_select_fusion
  62.7 0.1 compare_reduce_fusion.1
  62.8 0.1 broadcast_subtract_fusion
  62.9 1.7 compare_reduce_fusion
  64.6 0.1 broadcast_compare_fusion
  64.7 0.1 subtract_compare_fusion.1
  64.8 19.8 %all-to-all-done.2 = bf16[16,256,128]{2,1,0:T(8,128)(2,1)S(1)} async-done(((bf16[16,256,128]{2,1,0:T(8,128)(2,1)}), bf16[16,256,128]{2,1,0:T(8,128)(2,1)S(1)}, u32[]{:S(2)}, u32[]{:S(2)}) %all-to-all-start.2) | async-done | bytes 1048608 | tf_op jit(solution)/shard_map/all_to_all | solution.py:330
  84.5 6.0 %all-to-all-start.5 = ((bf16[16,128,256]{2,1,0:T(8,128)(2,1)}), bf16[16,128,256]{2,1,0:T(8,128)(2,1)S(1)}, u32[]{:S(2)}, u32[]{:S(2)}) async-start(bf16[16,128,256]{2,1,0:T(8,128)(2,1)} %get-tuple-element.10), calls=%async_computation.5 | async-start | bytes 2097152 | tf_op jit(solution)/shard_map/all_to_all | solution.py:330
  90.6 0.4 convert_reduce_fusion
  91.0 0.1 fusion.1
  91.1 1.2 select_reduce_fusion
  92.3 0.1 fusion.15
  92.4 2.0 collective-permute-start.1
  94.4 0.1 collective-permute-start
  94.5 0.7 reshape_squeeze.15.list_ref
  95.2 0.1 broadcast_select_fusion
  95.3 0.7 fusion.7
  96.1 17.4 %all-to-all-done.5 = bf16[16,128,256]{2,1,0:T(8,128)(2,1)S(1)} async-done(((bf16[16,128,256]{2,1,0:T(8,128)(2,1)}), bf16[16,128,256]{2,1,0:T(8,128)(2,1)S(1)}, u32[]{:S(2)}, u32[]{:S(2)}) %all-to-all-start.5) | async-done | bytes 1048608 | tf_op jit(solution)/shard_map/all_to_all | solution.py:330
  113.5 6.3 %all-to-all-start.3 = ((bf16[16,128,128]{2,1,0:T(8,128)(2,1)}), bf16[16,128,128]{2,1,0:T(8,128)(2,1)}, u32[]{:S(2)}, u32[]{:S(2)}) async-start(bf16[16,128,128]{2,1,0:T(8,128)(2,1)} %get-tuple-element.9), calls=%async_computation.3 | async-start | bytes 1048576 | tf_op jit(solution)/shard_map/all_to_all | solution.py:330
  119.7 0.6 slice_bitcast_fusion
  120.3 10.9 %collective-permute-done = bf16[16,256,128]{2,1,0:T(8,128)(2,1)} collective-permute-done((bf16[16,256,128]{2,1,0:T(8,128)(2,1)S(1)}, bf16[16,256,128]{2,1,0:T(8,128)(2,1)}, u32[]{:S(2)}, u32[]{:S(2)}) %collective-permute-start) | collective-permute-done | bytes 1048608 | tf_op jit(solution)/shard_map/ppermute | solution.py:326
  131.2 14.6 %attention.7 = bf16[2048,128]{1,0:T(8,128)(2,1)} custom-call(s32[8]{0:T(128)} %get-tuple-element.19.steps_ref, s32[1152]{0:T(1024)} %reshape_squeeze.15.list_ref, f32[136,128]{1,0:T(8,128)} %get-tuple-element.11.table_hbm, bf16[2048,256]{1,0:T(8,128)(2,1)} %bitcast.46, bf16[4096,128]{1,0:T(8,128)(2,1)} %bitcast.38, bf16[4096,128]{1,0:T(8,128)(2,1)} %bitcast.8.refs_1_, ...), custom_call_target="tpu_custom_call" | custom-call | flops 8589934592 | bytes 5242880 | tf_op jit(solution)/shard_map/attention/pallas_call | solution.py:168
  145.9 14.4 %all-to-all-start.7 = ((bf16[16,128,128]{2,1,0:T(8,128)(2,1)}), bf16[16,128,128]{2,1,0:T(8,128)(2,1)}, u32[]{:S(2)}, u32[]{:S(2)}) async-start(bf16[16,128,128]{2,1,0:T(8,128)(2,1)} %bitcast.51), calls=%async_computation.7 | async-start | bytes 1048576 | tf_op jit(solution)/shard_map/all_to_all | solution.py:330
  160.3 0.7 reshape_squeeze.14.list_ref
  160.9 0.7 reshape_squeeze.13.list_ref
  161.6 0.7 reshape_squeeze.12.list_ref
  162.3 24.0 %attention.6 = bf16[2048,128]{1,0:T(8,128)(2,1)} custom-call(s32[8]{0:T(128)} %get-tuple-element.20.steps_ref, s32[1152]{0:T(1024)} %reshape_squeeze.14.list_ref, f32[136,128]{1,0:T(8,128)} %get-tuple-element.13.table_hbm, bf16[2048,256]{1,0:T(8,128)(2,1)} %bitcast.47, bf16[4096,128]{1,0:T(8,128)(2,1)} %bitcast.39, bf16[4096,128]{1,0:T(8,128)(2,1)} %bitcast.8.refs_1_, ...), custom_call_target="tpu_custom_call" | custom-call | flops 8589934592 | bytes 5242880 | tf_op jit(solution)/shard_map/attention/pallas_call | solution.py:168
  186.3 6.3 %all-to-all-start.6 = ((bf16[16,128,128]{2,1,0:T(8,128)(2,1)}), bf16[16,128,128]{2,1,0:T(8,128)(2,1)}, u32[]{:S(2)}, u32[]{:S(2)}) async-start(bf16[16,128,128]{2,1,0:T(8,128)(2,1)} %bitcast.50), calls=%async_computation.6 | async-start | bytes 1048576 | tf_op jit(solution)/shard_map/all_to_all | solution.py:330
  192.6 21.7 %attention.4.refs_4_ = bf16[2048,256]{1,0:T(8,128)(2,1)} custom-call(s32[8]{0:T(128)} %get-tuple-element.21.steps_ref, s32[1152]{0:T(1024)} %reshape_squeeze.13.list_ref, f32[136,128]{1,0:T(8,128)} %get-tuple-element.12.table_hbm, bf16[2048,128]{1,0:T(8,128)(2,1)} %bitcast.13.q_hbm, bf16[4096,128]{1,0:T(8,128)(2,1)} %bitcast.40, ...), custom_call_target="tpu_custom_call" | custom-call | flops 8589934592 | bytes 5242880 | tf_op jit(solution)/shard_map/attention/pallas_call | solution.py:168
  214.3 26.4 %attention.5 = bf16[2048,256]{1,0:T(8,128)(2,1)} custom-call(s32[8]{0:T(128)} %get-tuple-element.22.steps_ref, s32[1152]{0:T(1024)} %reshape_squeeze.12.list_ref, f32[136,128]{1,0:T(8,128)} %get-tuple-element.14.table_hbm, bf16[2048,128]{1,0:T(8,128)(2,1)} %bitcast.49, bf16[4096,128]{1,0:T(8,128)(2,1)} %bitcast.41, ...), custom_call_target="tpu_custom_call", output_to_operand_aliasing={{}: (8, {})} | custom-call | flops 8589934592 | bytes 5242880 | tf_op jit(solution)/shard_map/attention/pallas_call | solution.py:168
  240.7 29.7 %all_to_all.40.refs_0_ = bf16[16,128,256]{2,1,0:T(8,128)(2,1)} all-to-all(bf16[16,128,256]{2,1,0:T(8,128)(2,1)} %bitcast.48), channel_id=1, replica_groups=mesh['rep'=2,'seq'=16] {'seq'}, dimensions={0} | all-to-all | bytes 2097152 | tf_op jit(solution)/shard_map/all_to_all | solution.py:330
  270.4 3.9 %unpack_answers.1 = bf16[128,8192]{1,0:T(8,128)(2,1)} custom-call(s32[1]{0:T(128)} %bitcast.flip_ref, bf16[16,128,256]{2,1,0:T(8,128)(2,1)} %all_to_all.40.refs_0_, bf16[16,128,128]{2,1,0:T(8,128)(2,1)} %all-to-all-done.6.refs_1_, bf16[16,128,128]{2,1,0:T(8,128)(2,1)} %all-to-all-done.7.refs_2_), custom_call_target="tpu_custom_call" | custom-call | tf_op jit(solution)/shard_map/unpack_answers/pallas_call | solution.py:307
  (21 shorter events, 0.1 us)
Async XLA Ops:
  3.8 23.4 %all-to-all-start = ((bf16[16,128,128]{2,1,0:T(8,128)(2,1)}), bf16[16,128,128]{2,1,0:T(8,128)(2,1)S(1)}, u32[]{:S(2)}, u32[]{:S(2)}) async-start(bf16[16,128,128]{2,1,0:T(8,128)(2,1)} %get-tuple-element.8), calls=%async_computation | async-start | bytes 1048576 | tf_op jit(solution)/shard_map/all_to_all | solution.py:330
  27.2 0.8 copy-start.3
  28.1 27.6 %all-to-all-start.1 = ((bf16[16,256,128]{2,1,0:T(8,128)(2,1)}), bf16[16,256,128]{2,1,0:T(8,128)(2,1)S(1)}, u32[]{:S(2)}, u32[]{:S(2)}) async-start(bf16[16,256,128]{2,1,0:T(8,128)(2,1)} %pack_cache.2), calls=%async_computation.1 | async-start | bytes 2097152 | tf_op jit(solution)/shard_map/all_to_all | solution.py:330
  32.0 29.6 %copy-start.5 = (s32[64]{0:T(128)S(1)}, s32[64]{0:T(128)}, u32[]{:S(2)}) copy-start(s32[64]{0:T(128)} %param.11) | copy-start | bytes 772
  32.0 29.7 %copy-start.6 = (s32[64]{0:T(128)S(1)}, s32[64]{0:T(128)}, u32[]{:S(2)}) copy-start(s32[64]{0:T(128)} %param.13) | copy-start | bytes 772
  32.0 29.7 %copy-start.4 = (s32[64,32]{0,1:T(8,128)S(1)}, s32[64,32]{0,1:T(8,128)}, u32[]{:S(2)}) copy-start(s32[64,32]{0,1:T(8,128)} %param.12) | copy-start | bytes 24580
  55.7 38.7 %copy-start = (bf16[16,256,128]{2,1,0:T(8,128)(2,1)}, bf16[16,256,128]{2,1,0:T(8,128)(2,1)S(1)}, u32[]{:S(2)}) copy-start(bf16[16,256,128]{2,1,0:T(8,128)(2,1)S(1)} %all-to-all-done.1) | copy-start | bytes 3145732
  55.7 28.8 %all-to-all-start.2 = ((bf16[16,256,128]{2,1,0:T(8,128)(2,1)}), bf16[16,256,128]{2,1,0:T(8,128)(2,1)S(1)}, u32[]{:S(2)}, u32[]{:S(2)}) async-start(bf16[16,256,128]{2,1,0:T(8,128)(2,1)} %pack_cache.3), calls=%async_computation.2 | async-start | bytes 2097152 | tf_op jit(solution)/shard_map/all_to_all | solution.py:330
  84.5 28.9 %copy-start.1 = (bf16[16,256,128]{2,1,0:T(8,128)(2,1)}, bf16[16,256,128]{2,1,0:T(8,128)(2,1)S(1)}, u32[]{:S(2)}) copy-start(bf16[16,256,128]{2,1,0:T(8,128)(2,1)S(1)} %all-to-all-done.2) | copy-start | bytes 3145732
  84.5 28.9 %all-to-all-start.5 = ((bf16[16,128,256]{2,1,0:T(8,128)(2,1)}), bf16[16,128,256]{2,1,0:T(8,128)(2,1)S(1)}, u32[]{:S(2)}, u32[]{:S(2)}) async-start(bf16[16,128,256]{2,1,0:T(8,128)(2,1)} %get-tuple-element.10), calls=%async_computation.5 | async-start | bytes 2097152 | tf_op jit(solution)/shard_map/all_to_all | solution.py:330
  92.4 27.9 %collective-permute-start.1 = (bf16[16,256,128]{2,1,0:T(8,128)(2,1)S(1)}, bf16[16,256,128]{2,1,0:T(8,128)(2,1)}, u32[]{:S(2)}, u32[]{:S(2)}) collective-permute-start(bf16[16,256,128]{2,1,0:T(8,128)(2,1)S(1)} %all-to-all-done.2), channel_id=1, source_target_pairs={{0,1},{1,0},{2,3},{3,2},{4,5},{5,4},{6,7},{7,6},{8,9},{9,8},{10,11... | collective-permute-start | bytes 3145736 | tf_op jit(solution)/shard_map/ppermute | solution.py:326
  94.4 36.9 %collective-permute-start = (bf16[16,256,128]{2,1,0:T(8,128)(2,1)S(1)}, bf16[16,256,128]{2,1,0:T(8,128)(2,1)}, u32[]{:S(2)}, u32[]{:S(2)}) collective-permute-start(bf16[16,256,128]{2,1,0:T(8,128)(2,1)S(1)} %all-to-all-done.1), channel_id=1, source_target_pairs={{0,1},{1,0},{2,3},{3,2},{4,5},{5,4},{6,7},{7,6},{8,9},{9,8},{10,11... | collective-permute-start | bytes 3145736 | tf_op jit(solution)/shard_map/ppermute | solution.py:326
  113.5 17.8 %copy-start.2 = (bf16[16,128,256]{2,1,0:T(8,128)(2,1)}, bf16[16,128,256]{2,1,0:T(8,128)(2,1)S(1)}, u32[]{:S(2)}) copy-start(bf16[16,128,256]{2,1,0:T(8,128)(2,1)S(1)} %all-to-all-done.5) | copy-start | bytes 3145732
  113.5 32.4 %all-to-all-start.3 = ((bf16[16,128,128]{2,1,0:T(8,128)(2,1)}), bf16[16,128,128]{2,1,0:T(8,128)(2,1)}, u32[]{:S(2)}, u32[]{:S(2)}) async-start(bf16[16,128,128]{2,1,0:T(8,128)(2,1)} %get-tuple-element.9), calls=%async_computation.3 | async-start | bytes 1048576 | tf_op jit(solution)/shard_map/all_to_all | solution.py:330
  145.9 40.4 %all-to-all-start.7 = ((bf16[16,128,128]{2,1,0:T(8,128)(2,1)}), bf16[16,128,128]{2,1,0:T(8,128)(2,1)}, u32[]{:S(2)}, u32[]{:S(2)}) async-start(bf16[16,128,128]{2,1,0:T(8,128)(2,1)} %bitcast.51), calls=%async_computation.7 | async-start | bytes 1048576 | tf_op jit(solution)/shard_map/all_to_all | solution.py:330
  186.3 54.4 %all-to-all-start.6 = ((bf16[16,128,128]{2,1,0:T(8,128)(2,1)}), bf16[16,128,128]{2,1,0:T(8,128)(2,1)}, u32[]{:S(2)}, u32[]{:S(2)}) async-start(bf16[16,128,128]{2,1,0:T(8,128)(2,1)} %bitcast.50), calls=%async_computation.6 | async-start | bytes 1048576 | tf_op jit(solution)/shard_map/all_to_all | solution.py:330

commit v2 on v1

--- a/solution.py
+++ b/solution.py
@@ -18,7 +18,8 @@
 HIDE = -1e30
 STEPS = 4
 SPAN = 4
-GROUP = 8
+PHASES = (2, 0, 1, 3)
+GROUP = 12
 
 
 def attention_kernel(factor, pieces, first, place, steps_ref, list_ref, table_hbm, q_hbm, *refs):
@@ -59,7 +60,7 @@
         return carry
 
     lax.fori_loop(0, tiles, prepare, 0)
-    for copy in loads:
+    for copy in loads[:pieces]:
         copy.wait()
 
     def sent(couple):
@@ -119,6 +120,12 @@
             s = jnp.where((row <= column) | (row >= rows), s, HIDE)
             s_even[x] = s
             parts.append(top_of(s))
+
+        @pl.when(couple == 0)
+        def _():
+            for copy in loads[pieces:]:
+                copy.wait()
+
         peaks = (jnp.full((1, rows), HIDE, jnp.float32),) * 2
         count = jnp.maximum(steps_ref[couple * 2], steps_ref[couple * 2 + 1])
 
@@ -195,11 +202,11 @@
     )(steps, entries, table, q, *keys, *values, *priors)
 
 
-def make_plan(natural, where_is, heads_at, heads, stretch, vertical, vert_count, slash, slash_count):
+def make_plan(natural, where_is, chosen_heads, stretch, vertical, vert_count, slash, slash_count):
     blocks = natural.shape[0]
     lanes = -(-stretch // LANES) * LANES
     tiles = stretch // SPAN
-    take = lambda x: lax.dynamic_slice_in_dim(x, heads_at, heads, 0)
+    take = lambda x: x[chosen_heads]
     verticals, live_vert, slashes, live_slash = take(vertical), take(vert_count), take(slash), take(slash_count)
     lane = jnp.arange(lanes, dtype=jnp.int32)
     tile = jnp.arange(tiles, dtype=jnp.int32)
@@ -261,60 +268,64 @@
     )(flip, x)
 
 
-def pack_queries(queries, devices, sizes, flip):
+def pack_queries(queries, devices, sizes, flip, order):
     rows, width = queries.shape
     heads = sum(sizes)
     some = devices // STEPS
 
-    def kernel(flip_ref, q_ref, *out_refs):
+    def kernel(flip_ref, order_ref, q_ref, *out_refs):
         for d in range(some):
-            head = 0
+            phase = 0
             for size, out_ref in zip(sizes, out_refs):
-                at = (d * heads + head) * HEAD_DIM
-                out_ref[seat(d, flip_ref[0])] = q_ref[:, at:at + size * HEAD_DIM]
-                head += size
+                for place in range(size):
+                    head = order_ref[(pl.program_id(0) * some + d) * heads + phase]
+                    at = pl.multiple_of((d * heads + head) * HEAD_DIM, HEAD_DIM)
+                    out_ref[seat(d, flip_ref[0]), :, place * HEAD_DIM:(place + 1) * HEAD_DIM] = q_ref[:, pl.ds(at, HEAD_DIM)]
+                    phase += 1
 
     return pl.pallas_call(
         kernel,
         out_shape=[jax.ShapeDtypeStruct((devices, rows, n * HEAD_DIM), queries.dtype) for n in sizes],
         grid_spec=pltpu.PrefetchScalarGridSpec(
-            num_scalar_prefetch=1,
+            num_scalar_prefetch=2,
             grid=(STEPS,),
-            in_specs=[pl.BlockSpec((rows, width // STEPS), lambda i, s: (0, i))],
-            out_specs=[pl.BlockSpec((some, rows, n * HEAD_DIM), lambda i, s: (i, 0, 0)) for n in sizes],
+            in_specs=[pl.BlockSpec((rows, width // STEPS), lambda i, s, o: (0, i))],
+            out_specs=[pl.BlockSpec((some, rows, n * HEAD_DIM), lambda i, s, o: (i, 0, 0)) for n in sizes],
         ),
         cost_estimate=pl.CostEstimate(flops=16 * queries.size, bytes_accessed=4 * queries.size, transcendentals=0),
         name="pack_queries",
-    )(flip, queries)
-
-
-def unpack_answers(answers, flip):
+    )(flip, order, queries)
+
+
+def unpack_answers(answers, flip, order):
     devices, rows, _ = answers[0].shape
     sizes = [x.shape[2] // HEAD_DIM for x in answers]
     heads = sum(sizes)
     some = devices // STEPS
     width = devices * heads * HEAD_DIM
 
-    def kernel(flip_ref, *refs):
+    def kernel(flip_ref, order_ref, *refs):
         out_ref = refs[-1]
         for d in range(some):
-            head = 0
+            phase = 0
             for size, in_ref in zip(sizes, refs):
-                at = (d * heads + head) * HEAD_DIM
-                out_ref[:, at:at + size * HEAD_DIM] = in_ref[seat(d, flip_ref[0])]
-                head += size
+                for place in range(size):
+                    head = order_ref[(pl.program_id(0) * some + d) * heads + phase]
+                    at = pl.multiple_of((d * heads + head) * HEAD_DIM, HEAD_DIM)
+                    out_ref[:, pl.ds(at, HEAD_DIM)] = in_ref[seat(d, flip_ref[0]), :, place * HEAD_DIM:(place + 1) * HEAD_DIM]
+                    phase += 1
 
     return pl.pallas_call(
         kernel,
         out_shape=jax.ShapeDtypeStruct((rows, width), answers[0].dtype),
         grid_spec=pltpu.PrefetchScalarGridSpec(
-            num_scalar_prefetch=1,
+            num_scalar_prefetch=2,
             grid=(STEPS,),
-            in_specs=[pl.BlockSpec((some, rows, n * HEAD_DIM), lambda i, s: (i, 0, 0)) for n in sizes],
-            out_specs=pl.BlockSpec((rows, width // STEPS), lambda i, s: (0, i)),
+            in_specs=[pl.BlockSpec((some, rows, n * HEAD_DIM), lambda i, s, o: (i, 0, 0)) for n in sizes],
+            out_specs=pl.BlockSpec((rows, width // STEPS), lambda i, s, o: (0, i)),
         ),
         name="unpack_answers",
-    )(flip, *answers)
+    )(flip, order, *answers)
 
 
 def swapped(x, bit):
@@ -336,6 +347,18 @@
 
 def answer_sizes(heads):
     return (heads - 2, 1, 1) if heads > 2 else (1,) * heads
+
+
+def served_order(vert_count, slash_count, heads, blocks, stretch):
+    free = (1 - vert_count / blocks) * (1 - slash_count / (blocks - stretch)) ** SPAN
+    free = free.reshape(-1, heads)
+    index = jnp.arange(heads, dtype=jnp.int32)
+    mine, other = free[:, :, None], free[:, None, :]
+    ahead = (other < mine) | ((other == mine) & (index[None, None, :] < index[None, :, None]))
+    rank = jnp.sum(ahead, axis=2, dtype=jnp.int32)
+    turns = PHASES if heads == len(PHASES) else range(heads)
+    ranks = jnp.stack([jnp.sum(jnp.where(rank == r, index, 0), axis=1) for r in turns], axis=1)
+    return ranks.astype(jnp.int32)
 
 
 def body(queries, keys, values, vertical, vert_count, slash, slash_count):
@@ -357,7 +380,11 @@
     all_keys = shared(own_keys)
     own_values = exchanged(pack_cache(values, sharers, flip))
     all_values = shared(own_values)
-    packed = pack_queries(queries, seq_count, asked_sizes(heads), flip)
+    blocks, stretch = seq_count * key_rows // BLOCK, seq_count * query_rows // BLOCK
+    order = served_order(vert_count, slash_count, heads, blocks, stretch)
+    mine = position * heads + lax.dynamic_index_in_dim(order, position, 0, keepdims=False)
+    order = order.reshape(-1)
+    packed = pack_queries(queries, seq_count, asked_sizes(heads), flip, order)
     asked = []
     for size, part in zip(asked_sizes(heads), packed):
         part = exchanged(part).reshape(seq_count * query_rows, -1)
@@ -374,7 +401,7 @@
         return (piece * seq_count + block // (piece_blocks * sharers)) * piece_blocks + block % piece_blocks
 
     table, entries, steps = make_plan(
-        natural, where_is, position * heads, heads, seq_count * query_rows // BLOCK,
+        natural, where_is, mine, stretch,
         vertical, vert_count, slash, slash_count,
     )
     plans = [(table[h], entries[h].reshape(-1), steps[h]) for h in range(heads)]
@@ -387,7 +414,7 @@
             found = attention(part, all_keys, all_values, *plans[head], h, place, size, found)
             head += 1
         answers.append(exchanged(found.reshape(seq_count, query_rows, size * HEAD_DIM)))
-    return unpack_answers(answers, flip)
+    return unpack_answers(answers, flip, order)
 
 
 def solution(mesh):

time: 276 us -> 272 us (0.986)
  local copies, waits for them, and re-layouts: 5.11 us -> 10.2 us
  starting transfers between devices: 53.2 us -> 48.4 us
    all_to_all x7, starting transfers between devices: 51.1 us -> 46.3 us  [exchanged(): return lax.all_to_all(x, 'seq', split_axis=0, concat_axis=0, tiled=True)]
  transfers between devices with their start and end apart: 9 -> 9, of which waited for: 5 -> 5; matrix products, arithmetic and copies ran while one was open for 3% -> 5% of each run, Pallas kernels for 34% -> 34%
where the time goes in v2:
time: 272 us; the launch traced here: 270 us
  Pallas kernels  101 us (37%)
  waiting for transfers between devices  77.5 us (28%)
  starting transfers between devices  48.4 us (18%)
  blocking collectives  27.1 us (10%)
  local copies, waits for them, and re-layouts  10.2 us (4%)
  other arithmetic  4.65 us (2%)
    pallas_call x4, Pallas kernels, attention(): pl.pallas_call(functools.partial(attention_kernel, factor, pieces, first,...  85.1 us
    all_to_all x7, waiting for transfers between devices, exchanged(): return lax.all_to_all(x, 'seq', split_axis=0, concat_axis=0, tiled=True)  66.6 us
    all_to_all x7, starting transfers between devices, exchanged(): return lax.all_to_all(x, 'seq', split_axis=0, concat_axis=0, tiled=True)  46.3 us
    all_to_all x1, blocking collectives, exchanged(): return lax.all_to_all(x, 'seq', split_axis=0, concat_axis=0, tiled=True)  27.1 us
    ppermute x2, waiting for transfers between devices, swapped(): return lax.ppermute(x, ('rep', 'seq'), moves)  10.9 us
    pallas_call x2, Pallas kernels, pack_cache(): pl.pallas_call(kernel, out_shape=jax.ShapeDtypeStruct((KV_HEADS * sharers...  6.83 us
  transfers between devices with their start and end apart: 9, of which 5 were waited for; matrix products, arithmetic and copies ran while one was open for 5% of the time, Pallas kernels for 34%

profile of v2, /device:TPU:0, one launch (start us, length us, event | category | flops | bytes accessed | tf_op | source)
XLA Modules:
  0.0 270.1 jit_solution(5016216037014574797)
XLA Ops:
  0.0 0.7 multiply_multiply_fusion
  0.9 0.1 convert_reduce_fusion.1
  1.0 0.1 copy.15
  1.1 0.6 reshape.504.order_ref
  1.7 4.6 %pack_queries.1 = (bf16[16,128,128]{2,1,0:T(8,128)(2,1)}, bf16[16,128,128]{2,1,0:T(8,128)(2,1)}, bf16[16,128,256]{2,1,0:T(8,128)(2,1)}) custom-call(s32[1]{0:T(128)} %bitcast.flip_ref, s32[64]{0:T(128)} %reshape.504.order_ref, bf16[128,8192]{1,0:T(8,128)(2,1)} %q_ref.1), custom_call_target="tpu_custom_call" | custom-call | flops 16777216 | bytes 4194304 | tf_op jit(solution)/shard_map/pack_queries/pallas_call | solution.py:286
  6.4 8.3 %all-to-all-start = ((bf16[16,128,128]{2,1,0:T(8,128)(2,1)}), bf16[16,128,128]{2,1,0:T(8,128)(2,1)S(1)}, u32[]{:S(2)}, u32[]{:S(2)}) async-start(bf16[16,128,128]{2,1,0:T(8,128)(2,1)} %get-tuple-element.8), calls=%async_computation | async-start | bytes 1048576 | tf_op jit(solution)/shard_map/all_to_all | solution.py:341
  14.7 3.4 %pack_cache.2 = bf16[16,256,128]{2,1,0:T(8,128)(2,1)} custom-call(s32[1]{0:T(128)} %bitcast.flip_ref, bf16[512,1024]{1,0:T(8,128)(2,1)} %in_ref.2), custom_call_target="tpu_custom_call" | custom-call | flops 8388608 | bytes 2097152 | tf_op jit(solution)/shard_map/pack_cache/pallas_call | solution.py:257
  18.1 11.7 %all-to-all-done = bf16[16,128,128]{2,1,0:T(8,128)(2,1)S(1)} async-done(((bf16[16,128,128]{2,1,0:T(8,128)(2,1)}), bf16[16,128,128]{2,1,0:T(8,128)(2,1)S(1)}, u32[]{:S(2)}, u32[]{:S(2)}) %all-to-all-start) | async-done | bytes 524320 | tf_op jit(solution)/shard_map/all_to_all | solution.py:341
  29.8 0.8 copy-done.6
  30.6 3.9 %all-to-all-start.1 = ((bf16[16,256,128]{2,1,0:T(8,128)(2,1)}), bf16[16,256,128]{2,1,0:T(8,128)(2,1)S(1)}, u32[]{:S(2)}, u32[]{:S(2)}) async-start(bf16[16,256,128]{2,1,0:T(8,128)(2,1)} %pack_cache.2), calls=%async_computation.1 | async-start | bytes 2097152 | tf_op jit(solution)/shard_map/all_to_all | solution.py:341
  34.6 0.2 add_reduce_fusion
  34.8 3.4 %pack_cache.3 = bf16[16,256,128]{2,1,0:T(8,128)(2,1)} custom-call(s32[1]{0:T(128)} %bitcast.flip_ref, bf16[512,1024]{1,0:T(8,128)(2,1)} %in_ref.3), custom_call_target="tpu_custom_call" | custom-call | flops 8388608 | bytes 2097152 | tf_op jit(solution)/shard_map/pack_cache/pallas_call | solution.py:257
  38.2 20.0 %all-to-all-done.1 = bf16[16,256,128]{2,1,0:T(8,128)(2,1)S(1)} async-done(((bf16[16,256,128]{2,1,0:T(8,128)(2,1)}), bf16[16,256,128]{2,1,0:T(8,128)(2,1)S(1)}, u32[]{:S(2)}, u32[]{:S(2)}) %all-to-all-start.1) | async-done | bytes 1048608 | tf_op jit(solution)/shard_map/all_to_all | solution.py:341
  58.2 5.9 %all-to-all-start.2 = ((bf16[16,256,128]{2,1,0:T(8,128)(2,1)}), bf16[16,256,128]{2,1,0:T(8,128)(2,1)S(1)}, u32[]{:S(2)}, u32[]{:S(2)}) async-start(bf16[16,256,128]{2,1,0:T(8,128)(2,1)} %pack_cache.3), calls=%async_computation.2 | async-start | bytes 2097152 | tf_op jit(solution)/shard_map/all_to_all | solution.py:341
  64.1 0.6 gather_fusion.2
  64.8 0.6 gather_fusion
  65.4 0.6 gather_fusion.1
  66.1 0.6 gather_fusion.3
  66.8 0.1 compare_reduce_fusion.1
  67.0 1.7 compare_reduce_fusion
  68.8 0.1 subtract_compare_fusion.1
  68.9 18.2 %all-to-all-done.2 = bf16[16,256,128]{2,1,0:T(8,128)(2,1)S(1)} async-done(((bf16[16,256,128]{2,1,0:T(8,128)(2,1)}), bf16[16,256,128]{2,1,0:T(8,128)(2,1)S(1)}, u32[]{:S(2)}, u32[]{:S(2)}) %all-to-all-start.2) | async-done | bytes 1048608 | tf_op jit(solution)/shard_map/all_to_all | solution.py:341
  87.1 6.0 %all-to-all-start.5 = ((bf16[16,128,256]{2,1,0:T(8,128)(2,1)}), bf16[16,128,256]{2,1,0:T(8,128)(2,1)S(1)}, u32[]{:S(2)}, u32[]{:S(2)}) async-start(bf16[16,128,256]{2,1,0:T(8,128)(2,1)} %get-tuple-element.10), calls=%async_computation.5 | async-start | bytes 2097152 | tf_op jit(solution)/shard_map/all_to_all | solution.py:341
  93.1 0.4 convert_reduce_fusion
  93.5 0.1 fusion.1
  93.7 1.2 select_reduce_fusion
  94.8 0.1 fusion.15
  94.9 2.0 collective-permute-start.1
  96.9 0.1 collective-permute-start
  97.0 0.6 fusion.34
  97.6 0.7 reshape_squeeze.15.list_ref
  98.3 0.1 broadcast_select_fusion
  98.4 0.7 fusion.7
  99.2 16.8 %all-to-all-done.5 = bf16[16,128,256]{2,1,0:T(8,128)(2,1)S(1)} async-done(((bf16[16,128,256]{2,1,0:T(8,128)(2,1)}), bf16[16,128,256]{2,1,0:T(8,128)(2,1)S(1)}, u32[]{:S(2)}, u32[]{:S(2)}) %all-to-all-start.5) | async-done | bytes 1048608 | tf_op jit(solution)/shard_map/all_to_all | solution.py:341
  116.0 6.3 %all-to-all-start.3 = ((bf16[16,128,128]{2,1,0:T(8,128)(2,1)}), bf16[16,128,128]{2,1,0:T(8,128)(2,1)}, u32[]{:S(2)}, u32[]{:S(2)}) async-start(bf16[16,128,128]{2,1,0:T(8,128)(2,1)} %get-tuple-element.9), calls=%async_computation.3 | async-start | bytes 1048576 | tf_op jit(solution)/shard_map/all_to_all | solution.py:341
  122.3 0.6 slice_bitcast_fusion
  122.9 10.9 %collective-permute-done = bf16[16,256,128]{2,1,0:T(8,128)(2,1)} collective-permute-done((bf16[16,256,128]{2,1,0:T(8,128)(2,1)S(1)}, bf16[16,256,128]{2,1,0:T(8,128)(2,1)}, u32[]{:S(2)}, u32[]{:S(2)}) %collective-permute-start) | collective-permute-done | bytes 1048608 | tf_op jit(solution)/shard_map/ppermute | solution.py:337
  133.8 15.1 %attention.7 = bf16[2048,128]{1,0:T(8,128)(2,1)} custom-call(s32[8]{0:T(128)} %get-tuple-element.23.steps_ref, s32[1216]{0:T(1024)} %reshape_squeeze.15.list_ref, f32[136,128]{1,0:T(8,128)} %get-tuple-element.15.table_hbm, bf16[2048,256]{1,0:T(8,128)(2,1)} %bitcast.54, bf16[4096,128]{1,0:T(8,128)(2,1)} %bitcast.46, bf16[4096,128]{1,0:T(8,128)(2,1)} %bitcast.13.refs_1_, ...), custom_call_target="tpu_custom_call" | custom-call | flops 8589934592 | bytes 5242880 | tf_op jit(solution)/shard_map/attention/pallas_call | solution.py:175
  148.9 10.3 %all-to-all-start.7 = ((bf16[16,128,128]{2,1,0:T(8,128)(2,1)}), bf16[16,128,128]{2,1,0:T(8,128)(2,1)}, u32[]{:S(2)}, u32[]{:S(2)}) async-start(bf16[16,128,128]{2,1,0:T(8,128)(2,1)} %bitcast.59), calls=%async_computation.7 | async-start | bytes 1048576 | tf_op jit(solution)/shard_map/all_to_all | solution.py:341
  159.2 1.4 reshape_squeeze.14.list_ref
  160.5 1.4 reshape_squeeze.13.list_ref
  161.9 0.7 reshape_squeeze.12.list_ref
  162.6 23.7 %attention.6 = bf16[2048,128]{1,0:T(8,128)(2,1)} custom-call(s32[8]{0:T(128)} %get-tuple-element.24.steps_ref, s32[1216]{0:T(1024)} %reshape_squeeze.14.list_ref, f32[136,128]{1,0:T(8,128)} %get-tuple-element.17.table_hbm, bf16[2048,256]{1,0:T(8,128)(2,1)} %bitcast.55, bf16[4096,128]{1,0:T(8,128)(2,1)} %bitcast.47, bf16[4096,128]{1,0:T(8,128)(2,1)} %bitcast.13.refs_1_, ...), custom_call_target="tpu_custom_call" | custom-call | flops 8589934592 | bytes 5242880 | tf_op jit(solution)/shard_map/attention/pallas_call | solution.py:175
  186.4 5.6 %all-to-all-start.6 = ((bf16[16,128,128]{2,1,0:T(8,128)(2,1)}), bf16[16,128,128]{2,1,0:T(8,128)(2,1)}, u32[]{:S(2)}, u32[]{:S(2)}) async-start(bf16[16,128,128]{2,1,0:T(8,128)(2,1)} %bitcast.58), calls=%async_computation.6 | async-start | bytes 1048576 | tf_op jit(solution)/shard_map/all_to_all | solution.py:341
  191.9 21.2 %attention.4.refs_4_ = bf16[2048,256]{1,0:T(8,128)(2,1)} custom-call(s32[8]{0:T(128)} %get-tuple-element.25.steps_ref, s32[1216]{0:T(1024)} %reshape_squeeze.13.list_ref, f32[136,128]{1,0:T(8,128)} %get-tuple-element.16.table_hbm, bf16[2048,128]{1,0:T(8,128)(2,1)} %bitcast.18.q_hbm, bf16[4096,128]{1,0:T(8,128)(2,1)} %bitcast.48, ...), custom_call_target="tpu_custom_call" | custom-call | flops 8589934592 | bytes 5242880 | tf_op jit(solution)/shard_map/attention/pallas_call | solution.py:175
  213.1 25.1 %attention.5 = bf16[2048,256]{1,0:T(8,128)(2,1)} custom-call(s32[8]{0:T(128)} %get-tuple-element.26.steps_ref, s32[1216]{0:T(1024)} %reshape_squeeze.12.list_ref, f32[136,128]{1,0:T(8,128)} %get-tuple-element.18.table_hbm, bf16[2048,128]{1,0:T(8,128)(2,1)} %bitcast.57, bf16[4096,128]{1,0:T(8,128)(2,1)} %bitcast.49, ...), custom_call_target="tpu_custom_call", output_to_operand_aliasing={{}: (8, {})} | custom-call | flops 8589934592 | bytes 5242880 | tf_op jit(solution)/shard_map/attention/pallas_call | solution.py:175
  238.2 27.1 %all_to_all.40.refs_0_ = bf16[16,128,256]{2,1,0:T(8,128)(2,1)} all-to-all(bf16[16,128,256]{2,1,0:T(8,128)(2,1)} %bitcast.56), channel_id=1, replica_groups=mesh['rep'=2,'seq'=16] {'seq'}, dimensions={0} | all-to-all | bytes 2097152 | tf_op jit(solution)/shard_map/all_to_all | solution.py:341
  265.4 4.7 %unpack_answers.1 = bf16[128,8192]{1,0:T(8,128)(2,1)} custom-call(s32[1]{0:T(128)} %bitcast.flip_ref, s32[64]{0:T(128)} %reshape.504.order_ref, bf16[16,128,256]{2,1,0:T(8,128)(2,1)} %all_to_all.40.refs_0_, bf16[16,128,128]{2,1,0:T(8,128)(2,1)} %all-to-all-done.6.refs_1_, bf16[16,128,128]{2,1,0:T(8,128)(2,1)} %all-to-all-done.7.refs_2_), custom_call_target="tpu_custom_call" | custom-call | tf_op jit(solution)/shard_map/unpack_answers/pallas_call | solution.py:318
  (37 shorter events, 0.7 us)
Async XLA Ops:
  0.0 65.4 %copy-start = (s32[64,64]{1,0:T(8,128)S(1)}, s32[64,64]{1,0:T(8,128)}, u32[]{:S(2)}) copy-start(s32[64,64]{1,0:T(8,128)} %param.10) | copy-start | bytes 49156
  6.4 23.4 %all-to-all-start = ((bf16[16,128,128]{2,1,0:T(8,128)(2,1)}), bf16[16,128,128]{2,1,0:T(8,128)(2,1)S(1)}, u32[]{:S(2)}, u32[]{:S(2)}) async-start(bf16[16,128,128]{2,1,0:T(8,128)(2,1)} %get-tuple-element.8), calls=%async_computation | async-start | bytes 1048576 | tf_op jit(solution)/shard_map/all_to_all | solution.py:341
  29.8 0.8 copy-start.6
  30.6 27.6 %all-to-all-start.1 = ((bf16[16,256,128]{2,1,0:T(8,128)(2,1)}), bf16[16,256,128]{2,1,0:T(8,128)(2,1)S(1)}, u32[]{:S(2)}, u32[]{:S(2)}) async-start(bf16[16,256,128]{2,1,0:T(8,128)(2,1)} %pack_cache.2), calls=%async_computation.1 | async-start | bytes 2097152 | tf_op jit(solution)/shard_map/all_to_all | solution.py:341
  34.8 29.4 %copy-start.1 = (s32[64]{0:T(128)S(1)}, s32[64]{0:T(128)}, u32[]{:S(2)}) copy-start(s32[64]{0:T(128)} %param.13) | copy-start | bytes 772
  34.8 30.0 %copy-start.2 = (s32[64]{0:T(128)S(1)}, s32[64]{0:T(128)}, u32[]{:S(2)}) copy-start(s32[64]{0:T(128)} %param.11) | copy-start | bytes 772
  38.2 27.8 %copy-start.7 = (s32[64,32]{0,1:T(8,128)S(1)}, s32[64,32]{0,1:T(8,128)}, u32[]{:S(2)}) copy-start(s32[64,32]{0,1:T(8,128)} %param.12) | copy-start | bytes 24580
  58.2 38.7 %copy-start.3 = (bf16[16,256,128]{2,1,0:T(8,128)(2,1)}, bf16[16,256,128]{2,1,0:T(8,128)(2,1)S(1)}, u32[]{:S(2)}) copy-start(bf16[16,256,128]{2,1,0:T(8,128)(2,1)S(1)} %all-to-all-done.1) | copy-start | bytes 3145732
  58.2 28.8 %all-to-all-start.2 = ((bf16[16,256,128]{2,1,0:T(8,128)(2,1)}), bf16[16,256,128]{2,1,0:T(8,128)(2,1)S(1)}, u32[]{:S(2)}, u32[]{:S(2)}) async-start(bf16[16,256,128]{2,1,0:T(8,128)(2,1)} %pack_cache.3), calls=%async_computation.2 | async-start | bytes 2097152 | tf_op jit(solution)/shard_map/all_to_all | solution.py:341
  87.1 28.9 %copy-start.4 = (bf16[16,256,128]{2,1,0:T(8,128)(2,1)}, bf16[16,256,128]{2,1,0:T(8,128)(2,1)S(1)}, u32[]{:S(2)}) copy-start(bf16[16,256,128]{2,1,0:T(8,128)(2,1)S(1)} %all-to-all-done.2) | copy-start | bytes 3145732
  87.1 28.9 %all-to-all-start.5 = ((bf16[16,128,256]{2,1,0:T(8,128)(2,1)}), bf16[16,128,256]{2,1,0:T(8,128)(2,1)S(1)}, u32[]{:S(2)}, u32[]{:S(2)}) async-start(bf16[16,128,256]{2,1,0:T(8,128)(2,1)} %get-tuple-element.10), calls=%async_computation.5 | async-start | bytes 2097152 | tf_op jit(solution)/shard_map/all_to_all | solution.py:341
  94.9 28.0 %collective-permute-start.1 = (bf16[16,256,128]{2,1,0:T(8,128)(2,1)S(1)}, bf16[16,256,128]{2,1,0:T(8,128)(2,1)}, u32[]{:S(2)}, u32[]{:S(2)}) collective-permute-start(bf16[16,256,128]{2,1,0:T(8,128)(2,1)S(1)} %all-to-all-done.2), channel_id=1, source_target_pairs={{0,1},{1,0},{2,3},{3,2},{4,5},{5,4},{6,7},{7,6},{8,9},{9,8},{10,11... | collective-permute-start | bytes 3145736 | tf_op jit(solution)/shard_map/ppermute | solution.py:337
  96.9 36.9 %collective-permute-start = (bf16[16,256,128]{2,1,0:T(8,128)(2,1)S(1)}, bf16[16,256,128]{2,1,0:T(8,128)(2,1)}, u32[]{:S(2)}, u32[]{:S(2)}) collective-permute-start(bf16[16,256,128]{2,1,0:T(8,128)(2,1)S(1)} %all-to-all-done.1), channel_id=1, source_target_pairs={{0,1},{1,0},{2,3},{3,2},{4,5},{5,4},{6,7},{7,6},{8,9},{9,8},{10,11... | collective-permute-start | bytes 3145736 | tf_op jit(solution)/shard_map/ppermute | solution.py:337
  116.0 17.8 %copy-start.5 = (bf16[16,128,256]{2,1,0:T(8,128)(2,1)}, bf16[16,128,256]{2,1,0:T(8,128)(2,1)S(1)}, u32[]{:S(2)}) copy-start(bf16[16,128,256]{2,1,0:T(8,128)(2,1)S(1)} %all-to-all-done.5) | copy-start | bytes 3145732
  116.0 32.9 %all-to-all-start.3 = ((bf16[16,128,128]{2,1,0:T(8,128)(2,1)}), bf16[16,128,128]{2,1,0:T(8,128)(2,1)}, u32[]{:S(2)}, u32[]{:S(2)}) async-start(bf16[16,128,128]{2,1,0:T(8,128)(2,1)} %get-tuple-element.9), calls=%async_computation.3 | async-start | bytes 1048576 | tf_op jit(solution)/shard_map/all_to_all | solution.py:341
  148.9 37.5 %all-to-all-start.7 = ((bf16[16,128,128]{2,1,0:T(8,128)(2,1)}), bf16[16,128,128]{2,1,0:T(8,128)(2,1)}, u32[]{:S(2)}, u32[]{:S(2)}) async-start(bf16[16,128,128]{2,1,0:T(8,128)(2,1)} %bitcast.59), calls=%async_computation.7 | async-start | bytes 1048576 | tf_op jit(solution)/shard_map/all_to_all | solution.py:341
  186.4 51.9 %all-to-all-start.6 = ((bf16[16,128,128]{2,1,0:T(8,128)(2,1)}), bf16[16,128,128]{2,1,0:T(8,128)(2,1)}, u32[]{:S(2)}, u32[]{:S(2)}) async-start(bf16[16,128,128]{2,1,0:T(8,128)(2,1)} %bitcast.58), calls=%async_computation.6 | async-start | bytes 1048576 | tf_op jit(solution)/shard_map/all_to_all | solution.py:341

commit v3 on v2

--- a/solution.py
+++ b/solution.py
@@ -16,7 +16,7 @@
 LANES = 128
 ONES = 16
 HIDE = -1e30
-STEPS = 4
+STEPS = 2
 SPAN = 4
 PHASES = (2, 0, 1, 3)
 GROUP = 12
@@ -137,11 +137,16 @@
             peaks = fold(2 * i + 1, s_odd, peaks, parts_odd)
             return peaks, parts
 
-        peaks, parts = lax.fori_loop(0, count // 2, pair, (peaks, tuple(parts)))
+        peaks, parts = lax.fori_loop(0, (count - 1) // 2, pair, (peaks, tuple(parts)))
 
         @pl.when(count % 2 == 1)
         def _():
             fold(count - 1, s_even, peaks, parts)
+
+        @pl.when(count % 2 == 0)
+        def _():
+            parts_odd = score(count - 1, s_odd)
+            fold(count - 1, s_odd, fold(count - 2, s_even, peaks, parts), parts_odd)
 
         for x in both:
             answer = acc[x, :width, :] / acc[x, width:width + 1, :]

time: 272 us -> 261 us (0.960)
  Pallas kernels: 101 us -> 88.7 us
    pallas_call x4, Pallas kernels: 85.1 us -> 77.4 us  [attention(): pl.pallas_call(functools.partial(attention_kernel, factor, pieces, first,...]
  transfers between devices with their start and end apart: 9 -> 9, of which waited for: 5 -> 5; matrix products, arithmetic and copies ran while one was open for 5% -> 5% of each run, Pallas kernels for 34% -> 31%
where the time goes in v3:
time: 261 us; the launch traced here: 259 us
  Pallas kernels  88.7 us (34%)
  waiting for transfers between devices  80.1 us (31%)
  starting transfers between devices  48.3 us (19%)
  blocking collectives  26.7 us (10%)
  local copies, waits for them, and re-layouts  10.2 us (4%)
  other arithmetic  4.65 us (2%)
    pallas_call x4, Pallas kernels, attention(): pl.pallas_call(functools.partial(attention_kernel, factor, pieces, first,...  77.4 us
    all_to_all x7, waiting for transfers between devices, exchanged(): return lax.all_to_all(x, 'seq', split_axis=0, concat_axis=0, tiled=True)  69.2 us
    all_to_all x7, starting transfers between devices, exchanged(): return lax.all_to_all(x, 'seq', split_axis=0, concat_axis=0, tiled=True)  46.2 us
    all_to_all x1, blocking collectives, exchanged(): return lax.all_to_all(x, 'seq', split_axis=0, concat_axis=0, tiled=True)  26.7 us
    ppermute x2, waiting for transfers between devices, swapped(): return lax.ppermute(x, ('rep', 'seq'), moves)  10.9 us
  transfers between devices with their start and end apart: 9, of which 5 were waited for; matrix products, arithmetic and copies ran while one was open for 5% of the time, Pallas kernels for 31%

profile of v3, /device:TPU:0, one launch (start us, length us, event | category | flops | bytes accessed | tf_op | source)
XLA Modules:
  0.0 259.4 jit_solution(8776136838259777037)
XLA Ops:
  0.0 0.7 multiply_multiply_fusion
  0.9 0.1 convert_reduce_fusion.1
  1.0 0.1 copy.15
  1.1 0.6 reshape.504.order_ref
  1.7 3.5 %pack_queries.1 = (bf16[16,128,128]{2,1,0:T(8,128)(2,1)}, bf16[16,128,128]{2,1,0:T(8,128)(2,1)}, bf16[16,128,256]{2,1,0:T(8,128)(2,1)}) custom-call(s32[1]{0:T(128)} %bitcast.flip_ref, s32[64]{0:T(128)} %reshape.504.order_ref, bf16[128,8192]{1,0:T(8,128)(2,1)} %q_ref.1), custom_call_target="tpu_custom_call" | custom-call | flops 16777216 | bytes 4194304 | tf_op jit(solution)/shard_map/pack_queries/pallas_call | solution.py:291
  5.2 8.3 %all-to-all-start = ((bf16[16,128,128]{2,1,0:T(8,128)(2,1)}), bf16[16,128,128]{2,1,0:T(8,128)(2,1)S(1)}, u32[]{:S(2)}, u32[]{:S(2)}) async-start(bf16[16,128,128]{2,1,0:T(8,128)(2,1)} %get-tuple-element.8), calls=%async_computation | async-start | bytes 1048576 | tf_op jit(solution)/shard_map/all_to_all | solution.py:346
  13.6 2.1 pack_cache.2
  15.7 13.0 %all-to-all-done = bf16[16,128,128]{2,1,0:T(8,128)(2,1)S(1)} async-done(((bf16[16,128,128]{2,1,0:T(8,128)(2,1)}), bf16[16,128,128]{2,1,0:T(8,128)(2,1)S(1)}, u32[]{:S(2)}, u32[]{:S(2)}) %all-to-all-start) | async-done | bytes 524320 | tf_op jit(solution)/shard_map/all_to_all | solution.py:346
  28.6 0.8 copy-done.6
  29.4 3.9 %all-to-all-start.1 = ((bf16[16,256,128]{2,1,0:T(8,128)(2,1)}), bf16[16,256,128]{2,1,0:T(8,128)(2,1)S(1)}, u32[]{:S(2)}, u32[]{:S(2)}) async-start(bf16[16,256,128]{2,1,0:T(8,128)(2,1)} %pack_cache.2), calls=%async_computation.1 | async-start | bytes 2097152 | tf_op jit(solution)/shard_map/all_to_all | solution.py:346
  33.4 0.2 add_reduce_fusion
  33.6 2.2 pack_cache.3
  35.8 21.3 %all-to-all-done.1 = bf16[16,256,128]{2,1,0:T(8,128)(2,1)S(1)} async-done(((bf16[16,256,128]{2,1,0:T(8,128)(2,1)}), bf16[16,256,128]{2,1,0:T(8,128)(2,1)S(1)}, u32[]{:S(2)}, u32[]{:S(2)}) %all-to-all-start.1) | async-done | bytes 1048608 | tf_op jit(solution)/shard_map/all_to_all | solution.py:346
  57.1 5.9 %all-to-all-start.2 = ((bf16[16,256,128]{2,1,0:T(8,128)(2,1)}), bf16[16,256,128]{2,1,0:T(8,128)(2,1)S(1)}, u32[]{:S(2)}, u32[]{:S(2)}) async-start(bf16[16,256,128]{2,1,0:T(8,128)(2,1)} %pack_cache.3), calls=%async_computation.2 | async-start | bytes 2097152 | tf_op jit(solution)/shard_map/all_to_all | solution.py:346
  63.0 0.6 gather_fusion.2
  63.6 0.6 gather_fusion
  64.3 0.6 gather_fusion.1
  64.9 0.6 gather_fusion.3
  65.6 0.1 compare_reduce_fusion.1
  65.9 1.7 compare_reduce_fusion
  67.7 0.1 subtract_compare_fusion.1
  67.8 18.2 %all-to-all-done.2 = bf16[16,256,128]{2,1,0:T(8,128)(2,1)S(1)} async-done(((bf16[16,256,128]{2,1,0:T(8,128)(2,1)}), bf16[16,256,128]{2,1,0:T(8,128)(2,1)S(1)}, u32[]{:S(2)}, u32[]{:S(2)}) %all-to-all-start.2) | async-done | bytes 1048608 | tf_op jit(solution)/shard_map/all_to_all | solution.py:346
  85.9 6.0 %all-to-all-start.5 = ((bf16[16,128,256]{2,1,0:T(8,128)(2,1)}), bf16[16,128,256]{2,1,0:T(8,128)(2,1)S(1)}, u32[]{:S(2)}, u32[]{:S(2)}) async-start(bf16[16,128,256]{2,1,0:T(8,128)(2,1)} %get-tuple-element.10), calls=%async_computation.5 | async-start | bytes 2097152 | tf_op jit(solution)/shard_map/all_to_all | solution.py:346
  92.0 0.4 convert_reduce_fusion
  92.4 0.1 fusion.1
  92.5 1.2 select_reduce_fusion
  93.7 0.1 fusion.15
  93.8 2.0 collective-permute-start.1
  95.8 0.1 collective-permute-start
  95.9 0.6 fusion.34
  96.5 0.7 reshape_squeeze.15.list_ref
  97.1 0.1 broadcast_select_fusion
  97.3 0.7 fusion.7
  98.0 16.8 %all-to-all-done.5 = bf16[16,128,256]{2,1,0:T(8,128)(2,1)S(1)} async-done(((bf16[16,128,256]{2,1,0:T(8,128)(2,1)}), bf16[16,128,256]{2,1,0:T(8,128)(2,1)S(1)}, u32[]{:S(2)}, u32[]{:S(2)}) %all-to-all-start.5) | async-done | bytes 1048608 | tf_op jit(solution)/shard_map/all_to_all | solution.py:346
  114.8 6.3 %all-to-all-start.3 = ((bf16[16,128,128]{2,1,0:T(8,128)(2,1)}), bf16[16,128,128]{2,1,0:T(8,128)(2,1)}, u32[]{:S(2)}, u32[]{:S(2)}) async-start(bf16[16,128,128]{2,1,0:T(8,128)(2,1)} %get-tuple-element.9), calls=%async_computation.3 | async-start | bytes 1048576 | tf_op jit(solution)/shard_map/all_to_all | solution.py:346
  121.1 0.6 slice_bitcast_fusion
  121.7 10.9 %collective-permute-done = bf16[16,256,128]{2,1,0:T(8,128)(2,1)} collective-permute-done((bf16[16,256,128]{2,1,0:T(8,128)(2,1)S(1)}, bf16[16,256,128]{2,1,0:T(8,128)(2,1)}, u32[]{:S(2)}, u32[]{:S(2)}) %collective-permute-start) | collective-permute-done | bytes 1048608 | tf_op jit(solution)/shard_map/ppermute | solution.py:342
  132.6 13.7 %attention.7 = bf16[2048,128]{1,0:T(8,128)(2,1)} custom-call(s32[8]{0:T(128)} %get-tuple-element.23.steps_ref, s32[1216]{0:T(1024)} %reshape_squeeze.15.list_ref, f32[136,128]{1,0:T(8,128)} %get-tuple-element.15.table_hbm, bf16[2048,256]{1,0:T(8,128)(2,1)} %bitcast.54, bf16[4096,128]{1,0:T(8,128)(2,1)} %bitcast.46, bf16[4096,128]{1,0:T(8,128)(2,1)} %bitcast.13.refs_1_, ...), custom_call_target="tpu_custom_call" | custom-call | flops 8589934592 | bytes 5242880 | tf_op jit(solution)/shard_map/attention/pallas_call | solution.py:180
  146.3 10.0 %all-to-all-start.7 = ((bf16[16,128,128]{2,1,0:T(8,128)(2,1)}), bf16[16,128,128]{2,1,0:T(8,128)(2,1)}, u32[]{:S(2)}, u32[]{:S(2)}) async-start(bf16[16,128,128]{2,1,0:T(8,128)(2,1)} %bitcast.59), calls=%async_computation.7 | async-start | bytes 1048576 | tf_op jit(solution)/shard_map/all_to_all | solution.py:346
  156.4 1.4 reshape_squeeze.14.list_ref
  157.8 1.4 reshape_squeeze.13.list_ref
  159.1 0.7 reshape_squeeze.12.list_ref
  159.8 21.3 %attention.6 = bf16[2048,128]{1,0:T(8,128)(2,1)} custom-call(s32[8]{0:T(128)} %get-tuple-element.24.steps_ref, s32[1216]{0:T(1024)} %reshape_squeeze.14.list_ref, f32[136,128]{1,0:T(8,128)} %get-tuple-element.17.table_hbm, bf16[2048,256]{1,0:T(8,128)(2,1)} %bitcast.55, bf16[4096,128]{1,0:T(8,128)(2,1)} %bitcast.47, bf16[4096,128]{1,0:T(8,128)(2,1)} %bitcast.13.refs_1_, ...), custom_call_target="tpu_custom_call" | custom-call | flops 8589934592 | bytes 5242880 | tf_op jit(solution)/shard_map/attention/pallas_call | solution.py:180
  181.1 5.6 %all-to-all-start.6 = ((bf16[16,128,128]{2,1,0:T(8,128)(2,1)}), bf16[16,128,128]{2,1,0:T(8,128)(2,1)}, u32[]{:S(2)}, u32[]{:S(2)}) async-start(bf16[16,128,128]{2,1,0:T(8,128)(2,1)} %bitcast.58), calls=%async_computation.6 | async-start | bytes 1048576 | tf_op jit(solution)/shard_map/all_to_all | solution.py:346
  186.8 19.5 %attention.4.refs_4_ = bf16[2048,256]{1,0:T(8,128)(2,1)} custom-call(s32[8]{0:T(128)} %get-tuple-element.25.steps_ref, s32[1216]{0:T(1024)} %reshape_squeeze.13.list_ref, f32[136,128]{1,0:T(8,128)} %get-tuple-element.16.table_hbm, bf16[2048,128]{1,0:T(8,128)(2,1)} %bitcast.18.q_hbm, bf16[4096,128]{1,0:T(8,128)(2,1)} %bitcast.48, ...), custom_call_target="tpu_custom_call" | custom-call | flops 8589934592 | bytes 5242880 | tf_op jit(solution)/shard_map/attention/pallas_call | solution.py:180
  206.3 22.8 %attention.5 = bf16[2048,256]{1,0:T(8,128)(2,1)} custom-call(s32[8]{0:T(128)} %get-tuple-element.26.steps_ref, s32[1216]{0:T(1024)} %reshape_squeeze.12.list_ref, f32[136,128]{1,0:T(8,128)} %get-tuple-element.18.table_hbm, bf16[2048,128]{1,0:T(8,128)(2,1)} %bitcast.57, bf16[4096,128]{1,0:T(8,128)(2,1)} %bitcast.49, ...), custom_call_target="tpu_custom_call", output_to_operand_aliasing={{}: (8, {})} | custom-call | flops 8589934592 | bytes 5242880 | tf_op jit(solution)/shard_map/attention/pallas_call | solution.py:180
  229.2 26.7 %all_to_all.40.refs_0_ = bf16[16,128,256]{2,1,0:T(8,128)(2,1)} all-to-all(bf16[16,128,256]{2,1,0:T(8,128)(2,1)} %bitcast.56), channel_id=1, replica_groups=mesh['rep'=2,'seq'=16] {'seq'}, dimensions={0} | all-to-all | bytes 2097152 | tf_op jit(solution)/shard_map/all_to_all | solution.py:346
  255.9 3.5 %unpack_answers.1 = bf16[128,8192]{1,0:T(8,128)(2,1)} custom-call(s32[1]{0:T(128)} %bitcast.flip_ref, s32[64]{0:T(128)} %reshape.504.order_ref, bf16[16,128,256]{2,1,0:T(8,128)(2,1)} %all_to_all.40.refs_0_, bf16[16,128,128]{2,1,0:T(8,128)(2,1)} %all-to-all-done.6.refs_1_, bf16[16,128,128]{2,1,0:T(8,128)(2,1)} %all-to-all-done.7.refs_2_), custom_call_target="tpu_custom_call" | custom-call | tf_op jit(solution)/shard_map/unpack_answers/pallas_call | solution.py:323
  (37 shorter events, 0.7 us)
Async XLA Ops:
  0.0 64.3 %copy-start = (s32[64,64]{1,0:T(8,128)S(1)}, s32[64,64]{1,0:T(8,128)}, u32[]{:S(2)}) copy-start(s32[64,64]{1,0:T(8,128)} %param.10) | copy-start | bytes 49156
  5.2 23.4 %all-to-all-start = ((bf16[16,128,128]{2,1,0:T(8,128)(2,1)}), bf16[16,128,128]{2,1,0:T(8,128)(2,1)S(1)}, u32[]{:S(2)}, u32[]{:S(2)}) async-start(bf16[16,128,128]{2,1,0:T(8,128)(2,1)} %get-tuple-element.8), calls=%async_computation | async-start | bytes 1048576 | tf_op jit(solution)/shard_map/all_to_all | solution.py:346
  28.6 0.8 copy-start.6
  29.4 27.6 %all-to-all-start.1 = ((bf16[16,256,128]{2,1,0:T(8,128)(2,1)}), bf16[16,256,128]{2,1,0:T(8,128)(2,1)S(1)}, u32[]{:S(2)}, u32[]{:S(2)}) async-start(bf16[16,256,128]{2,1,0:T(8,128)(2,1)} %pack_cache.2), calls=%async_computation.1 | async-start | bytes 2097152 | tf_op jit(solution)/shard_map/all_to_all | solution.py:346
  33.6 29.4 %copy-start.1 = (s32[64]{0:T(128)S(1)}, s32[64]{0:T(128)}, u32[]{:S(2)}) copy-start(s32[64]{0:T(128)} %param.13) | copy-start | bytes 772
  33.6 30.0 %copy-start.2 = (s32[64]{0:T(128)S(1)}, s32[64]{0:T(128)}, u32[]{:S(2)}) copy-start(s32[64]{0:T(128)} %param.11) | copy-start | bytes 772
  35.8 29.1 %copy-start.7 = (s32[64,32]{0,1:T(8,128)S(1)}, s32[64,32]{0,1:T(8,128)}, u32[]{:S(2)}) copy-start(s32[64,32]{0,1:T(8,128)} %param.12) | copy-start | bytes 24580
  57.1 38.7 %copy-start.3 = (bf16[16,256,128]{2,1,0:T(8,128)(2,1)}, bf16[16,256,128]{2,1,0:T(8,128)(2,1)S(1)}, u32[]{:S(2)}) copy-start(bf16[16,256,128]{2,1,0:T(8,128)(2,1)S(1)} %all-to-all-done.1) | copy-start | bytes 3145732
  57.1 28.8 %all-to-all-start.2 = ((bf16[16,256,128]{2,1,0:T(8,128)(2,1)}), bf16[16,256,128]{2,1,0:T(8,128)(2,1)S(1)}, u32[]{:S(2)}, u32[]{:S(2)}) async-start(bf16[16,256,128]{2,1,0:T(8,128)(2,1)} %pack_cache.3), calls=%async_computation.2 | async-start | bytes 2097152 | tf_op jit(solution)/shard_map/all_to_all | solution.py:346
  85.9 28.9 %copy-start.4 = (bf16[16,256,128]{2,1,0:T(8,128)(2,1)}, bf16[16,256,128]{2,1,0:T(8,128)(2,1)S(1)}, u32[]{:S(2)}) copy-start(bf16[16,256,128]{2,1,0:T(8,128)(2,1)S(1)} %all-to-all-done.2) | copy-start | bytes 3145732
  85.9 28.9 %all-to-all-start.5 = ((bf16[16,128,256]{2,1,0:T(8,128)(2,1)}), bf16[16,128,256]{2,1,0:T(8,128)(2,1)S(1)}, u32[]{:S(2)}, u32[]{:S(2)}) async-start(bf16[16,128,256]{2,1,0:T(8,128)(2,1)} %get-tuple-element.10), calls=%async_computation.5 | async-start | bytes 2097152 | tf_op jit(solution)/shard_map/all_to_all | solution.py:346
  93.8 28.0 %collective-permute-start.1 = (bf16[16,256,128]{2,1,0:T(8,128)(2,1)S(1)}, bf16[16,256,128]{2,1,0:T(8,128)(2,1)}, u32[]{:S(2)}, u32[]{:S(2)}) collective-permute-start(bf16[16,256,128]{2,1,0:T(8,128)(2,1)S(1)} %all-to-all-done.2), channel_id=1, source_target_pairs={{0,1},{1,0},{2,3},{3,2},{4,5},{5,4},{6,7},{7,6},{8,9},{9,8},{10,11... | collective-permute-start | bytes 3145736 | tf_op jit(solution)/shard_map/ppermute | solution.py:342
  95.8 36.9 %collective-permute-start = (bf16[16,256,128]{2,1,0:T(8,128)(2,1)S(1)}, bf16[16,256,128]{2,1,0:T(8,128)(2,1)}, u32[]{:S(2)}, u32[]{:S(2)}) collective-permute-start(bf16[16,256,128]{2,1,0:T(8,128)(2,1)S(1)} %all-to-all-done.1), channel_id=1, source_target_pairs={{0,1},{1,0},{2,3},{3,2},{4,5},{5,4},{6,7},{7,6},{8,9},{9,8},{10,11... | collective-permute-start | bytes 3145736 | tf_op jit(solution)/shard_map/ppermute | solution.py:342
  114.8 17.8 %copy-start.5 = (bf16[16,128,256]{2,1,0:T(8,128)(2,1)}, bf16[16,128,256]{2,1,0:T(8,128)(2,1)S(1)}, u32[]{:S(2)}) copy-start(bf16[16,128,256]{2,1,0:T(8,128)(2,1)S(1)} %all-to-all-done.5) | copy-start | bytes 3145732
  114.8 31.5 %all-to-all-start.3 = ((bf16[16,128,128]{2,1,0:T(8,128)(2,1)}), bf16[16,128,128]{2,1,0:T(8,128)(2,1)}, u32[]{:S(2)}, u32[]{:S(2)}) async-start(bf16[16,128,128]{2,1,0:T(8,128)(2,1)} %get-tuple-element.9), calls=%async_computation.3 | async-start | bytes 1048576 | tf_op jit(solution)/shard_map/all_to_all | solution.py:346
  146.3 34.8 %all-to-all-start.7 = ((bf16[16,128,128]{2,1,0:T(8,128)(2,1)}), bf16[16,128,128]{2,1,0:T(8,128)(2,1)}, u32[]{:S(2)}, u32[]{:S(2)}) async-start(bf16[16,128,128]{2,1,0:T(8,128)(2,1)} %bitcast.59), calls=%async_computation.7 | async-start | bytes 1048576 | tf_op jit(solution)/shard_map/all_to_all | solution.py:346
  181.1 48.0 %all-to-all-start.6 = ((bf16[16,128,128]{2,1,0:T(8,128)(2,1)}), bf16[16,128,128]{2,1,0:T(8,128)(2,1)}, u32[]{:S(2)}, u32[]{:S(2)}) async-start(bf16[16,128,128]{2,1,0:T(8,128)(2,1)} %bitcast.58), calls=%async_computation.6 | async-start | bytes 1048576 | tf_op jit(solution)/shard_map/all_to_all | solution.py:346
